TPU v7x, 32 devices: a whole 2x2x4 slice. The times are simulated.
32 devices in a mesh: section: 2 (over x), dp: 16 (over z, y, core).
Axes of the slice: x: 2, y: 2, z: 4, core: 2. Of those that a mesh axis runs over, the one named last changes fastest.
Arguments:
- inputs: bfloat16 [4, 2048, 1536], P(None, 'dp'), may hold values from -6 to 6
- out_grad: bfloat16 [4, 2048, 1536], P(None, 'dp'), may hold values from -0.125 to 0.125
- guide_bin: int32 [4, 1], replicated, may hold values from 0 to 31
- time_step: int32 [4, 1], replicated, may hold values from 0 to 999
- guide_table: bfloat16 [32, 4608], replicated, may hold values from -3 to 3
- section_table: float32 [2, 3, 1536], P('section'), may hold values from -3 to 3
- value_weight: bfloat16 [2, 1536, 1536], P('section'), may hold values from -0.15625 to 0.15625
- proj_weight: bfloat16 [2, 1536, 1536], P('section'), may hold values from -0.15625 to 0.15625
Outputs:
- value_grad: float32 [2, 1536, 1536], P('section', 'dp')
- proj_grad: float32 [2, 1536, 1536], P('section', 'dp')
- table_grad: float32 [2, 3, 1536], P('section', None, 'dp')
All inputs are finite; a program needn't handle non-finite values.
Results may differ from a plain program's by a relative error of at most 0.017.
Values may be sent and summed in bfloat16 or wider, within the bound.
A program may use at most 128 MiB of HBM per device.

v0:
```python
import functools
import math

import jax
import jax.numpy as jnp
from jax import lax
from jax.experimental import pallas as pl
from jax.experimental.pallas import tpu as pltpu
from jax.sharding import PartitionSpec as P

NORM_FLOOR = 0.1


def shifted(value, axis, steps):
    count = lax.axis_size(axis)
    leading, last = (max(0, -steps), min(count, count - steps))
    return lax.ppermute(value, axis, [(source, source + steps) for source in range(leading, last)])


def normalize(hidden):
    centre = jnp.mean(hidden, axis=-1, keepdims=True)
    centred = hidden - centre
    spread = jnp.mean(centred * centred, axis=-1, keepdims=True)
    inverse = lax.rsqrt(spread + NORM_FLOOR)
    return (centred * inverse, inverse)


def conditions(guide_bin, time_step, guide_table):
    total = guide_table.shape[1]
    half = total // 2
    frequency = jnp.exp(-math.log(10000.0) * jnp.arange(half, dtype=jnp.float32) / half)
    angle = time_step.astype(jnp.float32)[..., None] * frequency
    waves = jnp.concatenate([jnp.sin(angle), jnp.cos(angle)], axis=-1)
    bin_count = guide_table.shape[0]
    onehot = (guide_bin[..., None] == jnp.arange(bin_count, dtype=jnp.int32)).astype(jnp.float32)
    picked = jnp.einsum(
        "msb,bw->msw", onehot, guide_table.astype(jnp.float32), precision=lax.Precision.HIGHEST
    )
    return picked + 0.5 * waves


def contract_rows(left, right):
    return lax.dot_general(
        left, right, (((0,), (0,)), ((), ())), preferred_element_type=jnp.float32
    )


def forward_block(block_in, modulation, value_weight, proj_weight):
    width = block_in.shape[1]
    hidden = block_in.astype(jnp.float32)
    normed, inverse = normalize(hidden)
    shift = modulation[:, :width]
    scale = modulation[:, width : 2 * width]
    gate = modulation[:, 2 * width :]
    modulated = (normed * (1.0 + scale) + shift).astype(jnp.bfloat16)
    values = jnp.dot(modulated, value_weight, preferred_element_type=jnp.float32).astype(
        jnp.bfloat16
    )
    projected = jnp.dot(values, proj_weight, preferred_element_type=jnp.float32)
    block_out = (hidden + gate * projected).astype(jnp.bfloat16)
    return (block_out, modulated, values, projected)


def backward_block(block_in, projected, upstream, modulation, value_weight, proj_weight):
    width = block_in.shape[1]
    hidden = block_in.astype(jnp.float32)
    normed, inverse = normalize(hidden)
    scale = modulation[:, width : 2 * width]
    gate = modulation[:, 2 * width :]
    grad_up = upstream.astype(jnp.float32)
    grad_proj = (gate * grad_up).astype(jnp.bfloat16)
    grad_values = lax.dot_general(
        grad_proj, proj_weight, (((1,), (1,)), ((), ())), preferred_element_type=jnp.float32
    ).astype(jnp.bfloat16)
    grad_mod = lax.dot_general(
        grad_values, value_weight, (((1,), (1,)), ((), ())), preferred_element_type=jnp.float32
    )
    part_table = jnp.stack(
        [
            jnp.sum(grad_mod, axis=0),
            jnp.sum(grad_mod * normed, axis=0),
            jnp.sum(grad_up * projected, axis=0),
        ]
    )
    grad_norm = grad_mod * (1.0 + scale)
    centre_grad = jnp.mean(grad_norm, axis=-1, keepdims=True)
    cross = jnp.mean(grad_norm * normed, axis=-1, keepdims=True)
    grad_in = grad_up + inverse * (grad_norm - centre_grad - normed * cross)
    return (grad_in.astype(jnp.bfloat16), grad_values, grad_proj, part_table)


def per_device_scan(
    inputs, out_grad, guide_bin, time_step, guide_table, section_table, value_weight, proj_weight
):
    sections = lax.axis_size("section")
    section_id = lax.axis_index("section")
    position = lax.axis_index("dp")
    group_size = lax.axis_size("dp")
    tok_dev = inputs.shape[1]
    width = inputs.shape[2]
    value_width = value_weight.shape[2]
    batches = inputs.shape[0]
    samples = guide_bin.shape[1]
    tokens = tok_dev * group_size
    rows_per = tokens // samples
    parts = 1
    unit_rows = tok_dev // parts
    units = batches * parts
    condition = conditions(guide_bin, time_step, guide_table)
    weights_value = value_weight[0]
    weights_proj = proj_weight[0]
    section_row = section_table[0].reshape(-1)
    sample_ids = jnp.arange(samples, dtype=jnp.int32)

    def unit_modulation(unit_id):
        batch_id = unit_id // parts
        piece_id = unit_id % parts
        chosen = lax.dynamic_index_in_dim(condition, batch_id, 0, keepdims=False)
        global_rows = (
            position * tok_dev + piece_id * unit_rows + jnp.arange(unit_rows, dtype=jnp.int32)
        )
        owner = global_rows // rows_per
        onehot = (owner[:, None] == sample_ids[None, :]).astype(jnp.float32)
        picked = jnp.dot(
            onehot, chosen, precision=lax.Precision.HIGHEST, preferred_element_type=jnp.float32
        )
        return picked + section_row

    slots = units + 1
    keep_in = jnp.zeros((slots, unit_rows, width), jnp.bfloat16)
    keep_mod = jnp.zeros((slots, unit_rows, width), jnp.bfloat16)
    keep_val = jnp.zeros((slots, unit_rows, value_width), jnp.bfloat16)
    keep_proj = jnp.zeros((slots, unit_rows, width), jnp.float32)
    arriving = jnp.zeros((unit_rows, width), jnp.bfloat16)

    def forward_tick(carry, tick_id):
        incoming, saved_in, saved_mod, saved_val, saved_proj = carry
        unit_id = tick_id - section_id
        valid = (unit_id >= 0) & (unit_id < units)
        clipped = jnp.clip(unit_id, 0, units - 1)
        first = lax.dynamic_index_in_dim(inputs, clipped, 0, keepdims=False)
        block_in = jnp.where(section_id == 0, first, incoming)

        def forward_active(operand):
            return forward_block(operand, unit_modulation(clipped), weights_value, weights_proj)

        def forward_resting(operand):
            return (
                jnp.zeros_like(operand),
                jnp.zeros_like(operand),
                jnp.zeros((unit_rows, value_width), jnp.bfloat16),
                jnp.zeros((unit_rows, width), jnp.float32),
            )

        block_out, modulated, values, projected = lax.cond(
            valid, forward_active, forward_resting, block_in
        )
        slot_id = jnp.where(valid, unit_id, units)
        saved_in = lax.dynamic_update_index_in_dim(saved_in, block_in, slot_id, 0)
        saved_mod = lax.dynamic_update_index_in_dim(saved_mod, modulated, slot_id, 0)
        saved_val = lax.dynamic_update_index_in_dim(saved_val, values, slot_id, 0)
        saved_proj = lax.dynamic_update_index_in_dim(saved_proj, projected, slot_id, 0)
        sent = shifted(block_out, "section", 1)
        return ((sent, saved_in, saved_mod, saved_val, saved_proj), None)

    ticks = jnp.arange(units + sections - 1, dtype=jnp.int32)
    carry, unused = lax.scan(
        forward_tick, (arriving, keep_in, keep_mod, keep_val, keep_proj), ticks
    )
    arriving, keep_in, keep_mod, keep_val, keep_proj = carry
    store = jnp.zeros((slots, unit_rows, value_width), jnp.bfloat16)
    extra_zero = jnp.zeros((unit_rows, value_width), jnp.bfloat16)
    keep_grad = jnp.zeros((slots, unit_rows, width), jnp.bfloat16)
    proj_sum = jnp.zeros((value_width, width), jnp.float32)
    table_sum = jnp.zeros((3, width), jnp.float32)

    def backward_tick(carry, tick_id):
        incoming, store_now, grads_now, proj_now, table_now = carry
        unit_id = tick_id - (sections - 1 - section_id)
        valid = (unit_id >= 0) & (unit_id < units)
        clipped = jnp.clip(unit_id, 0, units - 1)
        last = lax.dynamic_index_in_dim(out_grad, clipped, 0, keepdims=False)
        upstream = jnp.where(section_id == sections - 1, last, incoming)
        block_in = lax.dynamic_index_in_dim(keep_in, clipped, 0, keepdims=False)
        modulated = lax.dynamic_index_in_dim(keep_mod, clipped, 0, keepdims=False)
        values = lax.dynamic_index_in_dim(keep_val, clipped, 0, keepdims=False)
        projected = lax.dynamic_index_in_dim(keep_proj, clipped, 0, keepdims=False)

        def backward_active(operand):
            grad_in, grad_values, grad_proj, part_table = backward_block(
                block_in, projected, operand, unit_modulation(clipped), weights_value, weights_proj
            )
            part_proj = jnp.zeros((value_width, width), jnp.float32)
            return (grad_in, grad_values, grad_proj, part_proj, part_table)

        def backward_resting(operand):
            return (
                jnp.zeros_like(operand),
                extra_zero,
                jnp.zeros((unit_rows, width), jnp.bfloat16),
                jnp.zeros((value_width, width), jnp.float32),
                jnp.zeros((3, width), jnp.float32),
            )

        grad_in, extra, grad_proj, part_proj, part_table = lax.cond(
            valid, backward_active, backward_resting, upstream
        )
        slot_id = jnp.where(valid, unit_id, units)
        store_now = lax.dynamic_update_index_in_dim(store_now, extra, slot_id, 0)
        grads_now = lax.dynamic_update_index_in_dim(grads_now, grad_proj, slot_id, 0)
        sent = shifted(grad_in, "section", -1)
        return ((sent, store_now, grads_now, proj_now + part_proj, table_now + part_table), None)

    carry, unused = lax.scan(
        backward_tick, (arriving, store, keep_grad, proj_sum, table_sum), ticks
    )
    arriving, store, keep_grad, proj_sum, table_sum = carry
    mod_rows = keep_mod[:units].reshape(units * unit_rows, width)
    grad_rows = store[:units].reshape(units * unit_rows, value_width)
    columns = mod_rows
    value_part = lax.psum_scatter(
        contract_rows(columns, grad_rows), "dp", scatter_dimension=0, tiled=True
    )
    val_rows = keep_val[:units].reshape(units * unit_rows, value_width)
    upper_rows = keep_grad[:units].reshape(units * unit_rows, width)
    columns = val_rows
    proj_part = lax.psum_scatter(
        contract_rows(columns, upper_rows), "dp", scatter_dimension=0, tiled=True
    )
    table_part = lax.psum_scatter(table_sum, "dp", scatter_dimension=1, tiled=True)
    return (value_part[None], proj_part[None], table_part[None])


MESH = pl.DeviceIdType.MESH


def scatter_kernel(far, value_ref, proj_ref, table_ref, value_out, proj_out, table_out,
                   core_in, own, side_out, side_in, far_out, far_in, table_in,
                   core_send, core_recv, side_send, side_recv, far_send, far_recv,
                   table_send, table_recv):
    group = 4 * far
    me = lax.axis_index("dp")
    core, side, place = me % 2, (me // 2) % 2, me // 4
    barrier = pltpu.get_barrier_semaphore()
    for step in range(1, group):
        pl.semaphore_signal(
            barrier, inc=1, device_id={"dp": (me + step) % group}, device_id_type=MESH
        )
    pl.semaphore_wait(barrier, group - 1)

    matrices = (proj_ref, value_ref)
    offsets = [(far // 2 + step) % far for step in range(far)]
    offsets = [offset for offset in offsets if offset] + [0]
    pieces = [(matrix, slot) for matrix in range(2) for slot in range(far)]

    def row(slot, which_side, which_core):
        return (((place + offsets[slot]) % far) * 2 + which_side) * 2 + which_core

    core_copies = {}
    for turn in range(2):
        for index, (matrix, slot) in enumerate(pieces):
            which = (1 - side) if turn == 0 else side
            copy = pltpu.make_async_remote_copy(
                src_ref=matrices[matrix].at[row(slot, which, 1 - core)],
                dst_ref=core_in.at[turn, index],
                send_sem=core_send.at[turn, index],
                recv_sem=core_recv.at[turn, index],
                device_id={"dp": me - core + (1 - core)},
                device_id_type=MESH,
            )
            copy.start()
            core_copies[turn, index] = copy
    table_copies = []
    for step in range(1, group):
        copy = pltpu.make_async_remote_copy(
            src_ref=table_ref.at[(me + step) % group],
            dst_ref=table_in.at[step - 1],
            send_sem=table_send.at[step - 1],
            recv_sem=table_recv.at[step - 1],
            device_id={"dp": (me + step) % group},
            device_id_type=MESH,
        )
        copy.start()
        table_copies.append(copy)

    side_copies = []
    for index, (matrix, slot) in enumerate(pieces):
        core_copies[0, index].wait_recv()
        mine = matrices[matrix][row(slot, 1 - side, core)].astype(jnp.float32)
        side_out[index] = (mine + core_in[0, index].astype(jnp.float32)).astype(jnp.bfloat16)
        copy = pltpu.make_async_remote_copy(
            src_ref=side_out.at[index],
            dst_ref=side_in.at[index],
            send_sem=side_send.at[index],
            recv_sem=side_recv.at[index],
            device_id={"dp": me + 2 - 4 * side},
            device_id_type=MESH,
        )
        copy.start()
        side_copies.append(copy)
    far_copies = {}
    for index, (matrix, slot) in enumerate(pieces):
        core_copies[1, index].wait_recv()
        mine = matrices[matrix][row(slot, side, core)].astype(jnp.float32)
        mine = mine + core_in[1, index].astype(jnp.float32)
        side_copies[index].wait_recv()
        mine = mine + side_in[index].astype(jnp.float32)
        if offsets[slot] == 0:
            own[matrix] = mine
        else:
            far_out[index] = mine.astype(jnp.bfloat16)
            copy = pltpu.make_async_remote_copy(
                src_ref=far_out.at[index],
                dst_ref=far_in.at[index],
                send_sem=far_send.at[index],
                recv_sem=far_recv.at[index],
                device_id={"dp": (me + 4 * offsets[slot]) % group},
                device_id_type=MESH,
            )
            copy.start()
            far_copies[index] = copy
    total = table_ref[me]
    for step in range(1, group):
        table_copies[step - 1].wait_recv()
        total = total + table_in[step - 1]
    table_out[...] = total
    for matrix, out in enumerate((proj_out, value_out)):
        result = own[matrix]
        for index, (which, slot) in enumerate(pieces):
            if which == matrix and index in far_copies:
                far_copies[index].wait_recv()
                result = result + far_in[index].astype(jnp.float32)
        out[...] = result
    for copy in list(core_copies.values()) + table_copies + side_copies:
        copy.wait_send()
    for copy in far_copies.values():
        copy.wait_send()


def scatter_sums(value_part, proj_part, table_part):
    group = lax.axis_size("dp")
    far = group // 4
    rows, width = value_part.shape[0] // group, value_part.shape[1]
    table_rows, lanes = table_part.shape[0], table_part.shape[1] // group
    tables = table_part.reshape(table_rows, group, lanes).transpose(1, 0, 2)
    tables = jnp.pad(tables, ((0, 0), (0, -table_rows % 8), (0, -lanes % 128)))
    count = 2 * far
    block = (rows, width)
    vmem = pl.BlockSpec(memory_space=pltpu.VMEM)
    dma = pltpu.SemaphoreType.DMA
    value_sum, proj_sum, table_sum = pl.pallas_call(
        functools.partial(scatter_kernel, far),
        out_shape=(
            jax.ShapeDtypeStruct(block, jnp.float32),
            jax.ShapeDtypeStruct((value_part.shape[0] // group, proj_part.shape[1]), jnp.float32),
            jax.ShapeDtypeStruct(tables.shape[1:], jnp.float32),
        ),
        in_specs=[vmem] * 3,
        out_specs=(vmem,) * 3,
        scratch_shapes=[
            pltpu.VMEM((2, count) + block, jnp.bfloat16),
            pltpu.VMEM((2,) + block, jnp.float32),
            pltpu.VMEM((count,) + block, jnp.bfloat16),
            pltpu.VMEM((count,) + block, jnp.bfloat16),
            pltpu.VMEM((count,) + block, jnp.bfloat16),
            pltpu.VMEM((count,) + block, jnp.bfloat16),
            pltpu.VMEM((group - 1,) + tables.shape[1:], jnp.float32),
            dma((2, count)), dma((2, count)), dma((count,)), dma((count,)),
            dma((count,)), dma((count,)), dma((group - 1,)), dma((group - 1,)),
        ],
        compiler_params=pltpu.CompilerParams(
            collective_id=0, has_side_effects=True, vmem_limit_bytes=56 * 1024 * 1024
        ),
    )(
        value_part.reshape((group,) + block),
        proj_part.reshape((group,) + block),
        tables,
    )
    return value_sum, proj_sum, table_sum[:table_rows, :lanes]


def modulation_rows(guide_bin, time_step, guide_table, section_row, tok_dev):
    group_size = lax.axis_size("dp")
    position = lax.axis_index("dp")
    batches, samples = guide_bin.shape
    rows_per = tok_dev * group_size // samples
    if rows_per % tok_dev == 0:
        owner = (position * tok_dev) // rows_per
        guide_bin = lax.dynamic_slice_in_dim(guide_bin, owner, 1, 1)
        time_step = lax.dynamic_slice_in_dim(time_step, owner, 1, 1)
    kept = guide_bin.shape[1]
    total = guide_table.shape[1]
    half = total // 2
    frequency = jnp.exp(-math.log(10000.0) * jnp.arange(half, dtype=jnp.float32) / half)
    angle = time_step.reshape(-1, 1).astype(jnp.float32) * frequency
    waves = jnp.concatenate([jnp.sin(angle), jnp.cos(angle)], axis=-1)
    bins = jnp.arange(guide_table.shape[0], dtype=jnp.int32)
    picked = jnp.sum(
        jnp.where(
            (guide_bin.reshape(-1, 1) == bins)[:, :, None], guide_table.astype(jnp.float32), 0.0
        ),
        axis=1,
    )
    rows = (picked + 0.5 * waves + section_row).reshape(batches, kept, total)
    if kept == samples and samples > 1:
        owners = (position * tok_dev + jnp.arange(tok_dev, dtype=jnp.int32)) // rows_per
        rows = jnp.take(rows, owners, axis=1)
    return rows


def blocks_kernel(x_ref, up_ref, mod_ref, wv_ref, wp_ref, mod_out, val_out, gv_out, gp_out,
                  tab_out, proj_s, gm_s, send_s, arrive_s, send_sem, recv_sem):
    units, rows, width = x_ref.shape
    depth = wv_ref.shape[1]
    chunk = math.gcd(rows, 32)
    section = lax.axis_index("section")
    barrier = pltpu.get_barrier_semaphore()
    pl.semaphore_signal(
        barrier, inc=1, device_id={"section": 1 - section}, device_id_type=MESH
    )
    pl.semaphore_wait(barrier, 1)
    tab_out[...] = jnp.zeros_like(tab_out)

    def hop(unit):
        return pltpu.make_async_remote_copy(
            src_ref=send_s.at[unit],
            dst_ref=arrive_s.at[unit],
            send_sem=send_sem.at[unit],
            recv_sem=recv_sem.at[unit],
            device_id={"section": 1 - section},
            device_id_type=MESH,
        )

    def each_chunk(body):
        @pl.loop(0, rows // chunk)
        def step(index):
            body(pl.ds(pl.multiple_of(index * chunk, chunk), chunk))

    def multiply(size, body):
        tile = math.gcd(size, 512)

        @pl.loop(0, size // tile)
        def step(index):
            body(pl.ds(pl.multiple_of(index * tile, tile), tile))

    def add_rows(place, value):
        tab_out[place] += jnp.sum(value.reshape(chunk // 8, 8, width), axis=0)

    def forward(unit, source, send):
        def modulate(part):
            normed, inverse = normalize(source[unit, part].astype(jnp.float32))
            scaled = normed * (1.0 + mod_ref[unit, 1:2]) + mod_ref[unit, 0:1]
            mod_out[unit, part] = scaled.astype(jnp.bfloat16)

        def first_dot(part):
            val_out[unit, :, part] = jnp.dot(
                mod_out[unit], wv_ref[:, part], preferred_element_type=jnp.float32
            ).astype(jnp.bfloat16)

        def second_dot(part):
            proj_s[unit, :, part] = jnp.dot(
                val_out[unit], wp_ref[:, part], preferred_element_type=jnp.float32
            )

        def add_gated(part):
            hidden = source[unit, part].astype(jnp.float32)
            block_out = hidden + mod_ref[unit, 2:3] * proj_s[unit, part]
            send_s[unit, part] = block_out.astype(jnp.bfloat16)

        each_chunk(modulate)
        multiply(depth, first_dot)
        multiply(width, second_dot)
        if send:
            each_chunk(add_gated)

    def backward(unit, source, upstream, send):
        def gated(part):
            grad_up = upstream[unit, part].astype(jnp.float32)
            gp_out[unit, part] = (mod_ref[unit, 2:3] * grad_up).astype(jnp.bfloat16)
            add_rows(2, grad_up * proj_s[unit, part])

        def first_dot(part):
            gv_out[unit, :, part] = lax.dot_general(
                gp_out[unit], wp_ref[part, :], (((1,), (1,)), ((), ())),
                preferred_element_type=jnp.float32,
            ).astype(jnp.bfloat16)

        def second_dot(part):
            gm_s[:, part] = lax.dot_general(
                gv_out[unit], wv_ref[part, :], (((1,), (1,)), ((), ())),
                preferred_element_type=jnp.float32,
            )

        def to_input(part):
            normed, inverse = normalize(source[unit, part].astype(jnp.float32))
            grad_mod = gm_s[part]
            add_rows(0, grad_mod)
            add_rows(1, grad_mod * normed)
            if send:
                grad_norm = grad_mod * (1.0 + mod_ref[unit, 1:2])
                centre_grad = jnp.mean(grad_norm, axis=-1, keepdims=True)
                cross = jnp.mean(grad_norm * normed, axis=-1, keepdims=True)
                grad_up = upstream[unit, part].astype(jnp.float32)
                grad_in = grad_up + inverse * (grad_norm - centre_grad - normed * cross)
                send_s[unit, part] = grad_in.astype(jnp.bfloat16)

        each_chunk(gated)
        multiply(depth, first_dot)
        multiply(width, second_dot)
        each_chunk(to_input)

    @pl.when(section == 0)
    def earlier():
        @pl.loop(0, units)
        def out(unit):
            forward(unit, x_ref, True)
            hop(unit).start()

        @pl.loop(0, units)
        def back(unit):
            hop(unit).wait_recv()
            backward(unit, x_ref, arrive_s, False)

    @pl.when(section == 1)
    def later():
        @pl.loop(0, units)
        def both(unit):
            hop(unit).wait_recv()
            forward(unit, arrive_s, False)
            backward(unit, arrive_s, up_ref, True)
            hop(unit).start()

    @pl.loop(0, units)
    def finish(unit):
        hop(unit).wait_send()


def per_device(
    inputs, out_grad, guide_bin, time_step, guide_table, section_table, value_weight, proj_weight
):
    units, rows, width = inputs.shape
    depth = value_weight.shape[2]
    group = lax.axis_size("dp")
    per_sample = rows * group // guide_bin.shape[1]
    if lax.axis_size("section") != 2 or group % 4 or per_sample % rows or rows % 8:
        return per_device_scan(
            inputs, out_grad, guide_bin, time_step, guide_table, section_table,
            value_weight, proj_weight,
        )
    modulation = modulation_rows(
        guide_bin, time_step, guide_table, section_table[0].reshape(-1), rows
    ).reshape(units, 3, width)
    vmem = pl.BlockSpec(memory_space=pltpu.VMEM)
    wide = jax.ShapeDtypeStruct((units, rows, width), jnp.bfloat16)
    deep = jax.ShapeDtypeStruct((units, rows, depth), jnp.bfloat16)
    modulated, values, grad_values, grad_proj, tables = pl.pallas_call(
        blocks_kernel,
        out_shape=(wide, deep, deep, wide, jax.ShapeDtypeStruct((3, 8, width), jnp.float32)),
        in_specs=[vmem] * 5,
        out_specs=(vmem,) * 5,
        scratch_shapes=[
            pltpu.VMEM((units, rows, width), jnp.float32),
            pltpu.VMEM((rows, width), jnp.float32),
            pltpu.VMEM((units, rows, width), jnp.bfloat16),
            pltpu.VMEM((units, rows, width), jnp.bfloat16),
            pltpu.SemaphoreType.DMA((units,)),
            pltpu.SemaphoreType.DMA((units,)),
        ],
        compiler_params=pltpu.CompilerParams(
            collective_id=1, has_side_effects=True, vmem_limit_bytes=56 * 1024 * 1024
        ),
    )(inputs, out_grad, modulation, value_weight[0], proj_weight[0])
    count = units * rows
    value_part = contract_rows(
        modulated.reshape(count, width), grad_values.reshape(count, depth)
    ).astype(jnp.bfloat16)
    proj_part = contract_rows(
        values.reshape(count, depth), grad_proj.reshape(count, width)
    ).astype(jnp.bfloat16)
    value_sum, proj_sum, table_sum = scatter_sums(value_part, proj_part, jnp.sum(tables, axis=1))
    return (value_sum[None], proj_sum[None], table_sum[None])


def solution(mesh):
    return jax.shard_map(
        per_device,
        mesh=mesh,
        in_specs=(
            P(None, "dp", None),
            P(None, "dp", None),
            P(),
            P(),
            P(),
            P("section", None, None),
            P("section", None, None),
            P("section", None, None),
        ),
        out_specs=(P("section", "dp", None), P("section", "dp", None), P("section", None, "dp")),
        check_vma=False,
    )
```

profile of v0, /device:TPU:0, one launch (start us, length us, event | category | flops | bytes accessed | tf_op | source)
XLA Modules:
  0.0 164.9 jit_solution(9435571365589547592)
XLA Ops:
  0.6 0.7 iota_compare_fusion
  1.4 0.7 convert_bitcast_fusion
  2.0 0.7 copy.31
  2.8 0.3 multiply_sine_fusion
  3.1 1.0 convert_element_type.14
  4.1 0.4 select_reduce_fusion
  4.5 0.7 copy_add_fusion.mod_ref
  5.2 71.4 %shard_map.106 = (bf16[4,128,1536]{2,1,0:T(8,128)(2,1)}, bf16[4,128,1536]{2,1,0:T(8,128)(2,1)}, bf16[4,128,1536]{2,1,0:T(8,128)(2,1)}, bf16[4,128,1536]{2,1,0:T(8,128)(2,1)}, f32[3,8,1536]{2,1,0:T(8,128)}) custom-call(bf16[4,128,1536]{2,1,0:T(8,128)(2,1)} %x_ref.1, bf16[4,128,1536]{2,1,0:T(8,128)(2,1)} %up_ref.1, f32[4,3,1536]{2,1,0:T(4,128)} %copy_add_fusion.mod_ref, ...), custom_call_target="tpu_custom_call" | custom-call | tf_op jit(solution)/shard_map/pallas_call | solution.py:556
  76.6 1.0 reduce_sum.19
  77.5 0.1 reshape.59
  77.6 0.6 pad.4.table_ref
  78.3 0.0 copy-start.1
  78.3 0.0 copy-start.2
  78.3 6.8 %bitcast_convert_fusion.1 = bf16[1536,1536]{1,0:T(8,128)(2,1)} fusion(bf16[4,128,1536]{2,1,0:T(8,128)(2,1)} %get-tuple-element.11, bf16[4,128,1536]{2,1,0:T(8,128)(2,1)} %get-tuple-element.12), kind=kOutput, calls=%fused_computation.1 | convolution fusion | flops 2418278400 | bytes 7864320 | tf_op jit(solution)/shard_map/dot_general | solution.py:43
  85.1 0.0 copy-done.1
  85.1 0.0 copy-done.2
  85.1 4.4 %bitcast_convert_fusion = bf16[1536,1536]{1,0:T(8,128)(2,1)} fusion(bf16[4,128,1536]{2,1,0:T(8,128)(2,1)S(1)} %copy-done.1, bf16[4,128,1536]{2,1,0:T(8,128)(2,1)S(1)} %copy-done.2), kind=kOutput, calls=%fused_computation | convolution fusion | flops 2418278400 | bytes 7864320 | tf_op jit(solution)/shard_map/dot_general | solution.py:43
  89.4 71.4 %shard_map.107 = (f32[96,1536]{1,0:T(8,128)}, f32[96,1536]{1,0:T(8,128)}, f32[8,128]{1,0:T(8,128)}) custom-call(bf16[16,96,1536]{2,1,0:T(8,128)(2,1)} %bitcast.28, bf16[16,96,1536]{2,1,0:T(8,128)(2,1)} %bitcast.29, f32[16,8,128]{2,1,0:T(8,128)} %pad.4.table_ref), custom_call_target="tpu_custom_call" | custom-call | tf_op jit(solution)/shard_map/pallas_call | solution.py:351
  160.8 0.0 copy-start
  160.8 0.7 slice_bitcast_fusion
  161.6 0.6 copy.23
  162.1 1.9 %copy.34 = f32[1,96,1536]{2,1,0:T(8,128)} copy(f32[1,96,1536]{2,1,0:T(8,128)} %bitcast.31) | data formatting | bytes 1179648
  164.0 0.0 copy-done
  164.0 0.8 copy.35
  (3 shorter events, 0.1 us)
Async XLA Ops:
  78.3 6.8 %copy-start.1 = (bf16[4,128,1536]{2,1,0:T(8,128)(2,1)S(1)}, bf16[4,128,1536]{2,1,0:T(8,128)(2,1)}, u32[]{:S(2)}) copy-start(bf16[4,128,1536]{2,1,0:T(8,128)(2,1)} %get-tuple-element.13) | copy-start | bytes 4718596
  78.3 6.8 %copy-start.2 = (bf16[4,128,1536]{2,1,0:T(8,128)(2,1)S(1)}, bf16[4,128,1536]{2,1,0:T(8,128)(2,1)}, u32[]{:S(2)}) copy-start(bf16[4,128,1536]{2,1,0:T(8,128)(2,1)} %get-tuple-element.14) | copy-start | bytes 4718596
  160.8 3.2 %copy-start = (f32[96,1536]{1,0:T(8,128)S(1)}, f32[96,1536]{1,0:T(8,128)}, u32[]{:S(2)}) copy-start(f32[96,1536]{1,0:T(8,128)} %get-tuple-element.17) | copy-start | bytes 1769476
where the time goes:
time: 165 us
  Pallas kernels  143 us (87%)
  matrix products  11.2 us (7%)
  local copies, waits for them, and re-layouts  5.52 us (3%)
  other arithmetic  4.77 us (3%)
    pallas_call x1, Pallas kernels, scatter_sums(): pl.pallas_call(functools.partial(scatter_kernel, far), out_shape=(jax.Sha...  71.4 us
    pallas_call x1, Pallas kernels, per_device(): pl.pallas_call(blocks_kernel, out_shape=(wide, deep, deep, wide, jax.Shap...  71.4 us
    dot_general x2, matrix products, contract_rows(): lax.dot_general(left, right, (((0,), (0,)), ((), ())), preferred_element_...  11.2 us
    unnamed x10, local copies, waits for them, and re-layouts  4.04 us

commit v1 on v0

v1 whole, which is shorter than its diff:
```python
import functools
import math

import jax
import jax.numpy as jnp
from jax import lax
from jax.experimental import pallas as pl
from jax.experimental.pallas import tpu as pltpu
from jax.sharding import PartitionSpec as P

NORM_FLOOR = 0.1
PIECE_ROWS = 64


def shifted(value, axis, steps):
    count = lax.axis_size(axis)
    leading, last = (max(0, -steps), min(count, count - steps))
    return lax.ppermute(value, axis, [(source, source + steps) for source in range(leading, last)])


def normalize(hidden):
    centre = jnp.mean(hidden, axis=-1, keepdims=True)
    centred = hidden - centre
    spread = jnp.mean(centred * centred, axis=-1, keepdims=True)
    inverse = lax.rsqrt(spread + NORM_FLOOR)
    return (centred * inverse, inverse)


def conditions(guide_bin, time_step, guide_table):
    total = guide_table.shape[1]
    half = total // 2
    frequency = jnp.exp(-math.log(10000.0) * jnp.arange(half, dtype=jnp.float32) / half)
    angle = time_step.astype(jnp.float32)[..., None] * frequency
    waves = jnp.concatenate([jnp.sin(angle), jnp.cos(angle)], axis=-1)
    bin_count = guide_table.shape[0]
    onehot = (guide_bin[..., None] == jnp.arange(bin_count, dtype=jnp.int32)).astype(jnp.float32)
    picked = jnp.einsum(
        "msb,bw->msw", onehot, guide_table.astype(jnp.float32), precision=lax.Precision.HIGHEST
    )
    return picked + 0.5 * waves


def contract_rows(left, right):
    return lax.dot_general(
        left, right, (((0,), (0,)), ((), ())), preferred_element_type=jnp.float32
    )


def forward_block(block_in, modulation, value_weight, proj_weight):
    width = block_in.shape[1]
    hidden = block_in.astype(jnp.float32)
    normed, inverse = normalize(hidden)
    shift = modulation[:, :width]
    scale = modulation[:, width : 2 * width]
    gate = modulation[:, 2 * width :]
    modulated = (normed * (1.0 + scale) + shift).astype(jnp.bfloat16)
    values = jnp.dot(modulated, value_weight, preferred_element_type=jnp.float32).astype(
        jnp.bfloat16
    )
    projected = jnp.dot(values, proj_weight, preferred_element_type=jnp.float32)
    block_out = (hidden + gate * projected).astype(jnp.bfloat16)
    return (block_out, modulated, values, projected)


def backward_block(block_in, projected, upstream, modulation, value_weight, proj_weight):
    width = block_in.shape[1]
    hidden = block_in.astype(jnp.float32)
    normed, inverse = normalize(hidden)
    scale = modulation[:, width : 2 * width]
    gate = modulation[:, 2 * width :]
    grad_up = upstream.astype(jnp.float32)
    grad_proj = (gate * grad_up).astype(jnp.bfloat16)
    grad_values = lax.dot_general(
        grad_proj, proj_weight, (((1,), (1,)), ((), ())), preferred_element_type=jnp.float32
    ).astype(jnp.bfloat16)
    grad_mod = lax.dot_general(
        grad_values, value_weight, (((1,), (1,)), ((), ())), preferred_element_type=jnp.float32
    )
    part_table = jnp.stack(
        [
            jnp.sum(grad_mod, axis=0),
            jnp.sum(grad_mod * normed, axis=0),
            jnp.sum(grad_up * projected, axis=0),
        ]
    )
    grad_norm = grad_mod * (1.0 + scale)
    centre_grad = jnp.mean(grad_norm, axis=-1, keepdims=True)
    cross = jnp.mean(grad_norm * normed, axis=-1, keepdims=True)
    grad_in = grad_up + inverse * (grad_norm - centre_grad - normed * cross)
    return (grad_in.astype(jnp.bfloat16), grad_values, grad_proj, part_table)


def per_device_scan(
    inputs, out_grad, guide_bin, time_step, guide_table, section_table, value_weight, proj_weight
):
    sections = lax.axis_size("section")
    section_id = lax.axis_index("section")
    position = lax.axis_index("dp")
    group_size = lax.axis_size("dp")
    tok_dev = inputs.shape[1]
    width = inputs.shape[2]
    value_width = value_weight.shape[2]
    batches = inputs.shape[0]
    samples = guide_bin.shape[1]
    tokens = tok_dev * group_size
    rows_per = tokens // samples
    parts = 1
    unit_rows = tok_dev // parts
    units = batches * parts
    condition = conditions(guide_bin, time_step, guide_table)
    weights_value = value_weight[0]
    weights_proj = proj_weight[0]
    section_row = section_table[0].reshape(-1)
    sample_ids = jnp.arange(samples, dtype=jnp.int32)

    def unit_modulation(unit_id):
        batch_id = unit_id // parts
        piece_id = unit_id % parts
        chosen = lax.dynamic_index_in_dim(condition, batch_id, 0, keepdims=False)
        global_rows = (
            position * tok_dev + piece_id * unit_rows + jnp.arange(unit_rows, dtype=jnp.int32)
        )
        owner = global_rows // rows_per
        onehot = (owner[:, None] == sample_ids[None, :]).astype(jnp.float32)
        picked = jnp.dot(
            onehot, chosen, precision=lax.Precision.HIGHEST, preferred_element_type=jnp.float32
        )
        return picked + section_row

    slots = units + 1
    keep_in = jnp.zeros((slots, unit_rows, width), jnp.bfloat16)
    keep_mod = jnp.zeros((slots, unit_rows, width), jnp.bfloat16)
    keep_val = jnp.zeros((slots, unit_rows, value_width), jnp.bfloat16)
    keep_proj = jnp.zeros((slots, unit_rows, width), jnp.float32)
    arriving = jnp.zeros((unit_rows, width), jnp.bfloat16)

    def forward_tick(carry, tick_id):
        incoming, saved_in, saved_mod, saved_val, saved_proj = carry
        unit_id = tick_id - section_id
        valid = (unit_id >= 0) & (unit_id < units)
        clipped = jnp.clip(unit_id, 0, units - 1)
        first = lax.dynamic_index_in_dim(inputs, clipped, 0, keepdims=False)
        block_in = jnp.where(section_id == 0, first, incoming)

        def forward_active(operand):
            return forward_block(operand, unit_modulation(clipped), weights_value, weights_proj)

        def forward_resting(operand):
            return (
                jnp.zeros_like(operand),
                jnp.zeros_like(operand),
                jnp.zeros((unit_rows, value_width), jnp.bfloat16),
                jnp.zeros((unit_rows, width), jnp.float32),
            )

        block_out, modulated, values, projected = lax.cond(
            valid, forward_active, forward_resting, block_in
        )
        slot_id = jnp.where(valid, unit_id, units)
        saved_in = lax.dynamic_update_index_in_dim(saved_in, block_in, slot_id, 0)
        saved_mod = lax.dynamic_update_index_in_dim(saved_mod, modulated, slot_id, 0)
        saved_val = lax.dynamic_update_index_in_dim(saved_val, values, slot_id, 0)
        saved_proj = lax.dynamic_update_index_in_dim(saved_proj, projected, slot_id, 0)
        sent = shifted(block_out, "section", 1)
        return ((sent, saved_in, saved_mod, saved_val, saved_proj), None)

    ticks = jnp.arange(units + sections - 1, dtype=jnp.int32)
    carry, unused = lax.scan(
        forward_tick, (arriving, keep_in, keep_mod, keep_val, keep_proj), ticks
    )
    arriving, keep_in, keep_mod, keep_val, keep_proj = carry
    store = jnp.zeros((slots, unit_rows, value_width), jnp.bfloat16)
    extra_zero = jnp.zeros((unit_rows, value_width), jnp.bfloat16)
    keep_grad = jnp.zeros((slots, unit_rows, width), jnp.bfloat16)
    proj_sum = jnp.zeros((value_width, width), jnp.float32)
    table_sum = jnp.zeros((3, width), jnp.float32)

    def backward_tick(carry, tick_id):
        incoming, store_now, grads_now, proj_now, table_now = carry
        unit_id = tick_id - (sections - 1 - section_id)
        valid = (unit_id >= 0) & (unit_id < units)
        clipped = jnp.clip(unit_id, 0, units - 1)
        last = lax.dynamic_index_in_dim(out_grad, clipped, 0, keepdims=False)
        upstream = jnp.where(section_id == sections - 1, last, incoming)
        block_in = lax.dynamic_index_in_dim(keep_in, clipped, 0, keepdims=False)
        modulated = lax.dynamic_index_in_dim(keep_mod, clipped, 0, keepdims=False)
        values = lax.dynamic_index_in_dim(keep_val, clipped, 0, keepdims=False)
        projected = lax.dynamic_index_in_dim(keep_proj, clipped, 0, keepdims=False)

        def backward_active(operand):
            grad_in, grad_values, grad_proj, part_table = backward_block(
                block_in, projected, operand, unit_modulation(clipped), weights_value, weights_proj
            )
            part_proj = jnp.zeros((value_width, width), jnp.float32)
            return (grad_in, grad_values, grad_proj, part_proj, part_table)

        def backward_resting(operand):
            return (
                jnp.zeros_like(operand),
                extra_zero,
                jnp.zeros((unit_rows, width), jnp.bfloat16),
                jnp.zeros((value_width, width), jnp.float32),
                jnp.zeros((3, width), jnp.float32),
            )

        grad_in, extra, grad_proj, part_proj, part_table = lax.cond(
            valid, backward_active, backward_resting, upstream
        )
        slot_id = jnp.where(valid, unit_id, units)
        store_now = lax.dynamic_update_index_in_dim(store_now, extra, slot_id, 0)
        grads_now = lax.dynamic_update_index_in_dim(grads_now, grad_proj, slot_id, 0)
        sent = shifted(grad_in, "section", -1)
        return ((sent, store_now, grads_now, proj_now + part_proj, table_now + part_table), None)

    carry, unused = lax.scan(
        backward_tick, (arriving, store, keep_grad, proj_sum, table_sum), ticks
    )
    arriving, store, keep_grad, proj_sum, table_sum = carry
    mod_rows = keep_mod[:units].reshape(units * unit_rows, width)
    grad_rows = store[:units].reshape(units * unit_rows, value_width)
    columns = mod_rows
    value_part = lax.psum_scatter(
        contract_rows(columns, grad_rows), "dp", scatter_dimension=0, tiled=True
    )
    val_rows = keep_val[:units].reshape(units * unit_rows, value_width)
    upper_rows = keep_grad[:units].reshape(units * unit_rows, width)
    columns = val_rows
    proj_part = lax.psum_scatter(
        contract_rows(columns, upper_rows), "dp", scatter_dimension=0, tiled=True
    )
    table_part = lax.psum_scatter(table_sum, "dp", scatter_dimension=1, tiled=True)
    return (value_part[None], proj_part[None], table_part[None])


MESH = pl.DeviceIdType.MESH


def step_kernel(far, bin_ref, time_ref, guide_ref, section_ref, x_hbm, up_hbm, wv_hbm, wp_hbm,
                value_out, proj_out, table_out,
                x_s, up_s, wv_s, wp_s, rows_s, arrive_s, send_s, mod_s, val_s, left_s, right_s,
                proj_s, gm_s, tab_s, core_out, core_in, own_s, side_out, side_in, low_in, high_in,
                tables_s, tables_in, load_sem, hop_send, hop_recv, core_send, core_recv,
                side_send, side_recv, low_send, low_recv, high_send, high_recv,
                table_send, table_recv):
    units, unit_rows = x_hbm.shape[0], x_hbm.shape[1]
    count, width = x_s.shape
    depth = wv_s.shape[1]
    hops = hop_send.shape[0]
    piece = count // hops
    chunk = math.gcd(piece, 32)
    group = 4 * far
    section = lax.axis_index("section")
    me = lax.axis_index("dp")
    core, side, place = me % 2, (me // 2) % 2, me // 4

    barrier = pltpu.get_barrier_semaphore()
    pl.semaphore_signal(
        barrier, inc=1, device_id={"section": 1 - section}, device_id_type=MESH
    )
    for step in range(1, group):
        pl.semaphore_signal(
            barrier, inc=1, device_id={"dp": (me + step) % group}, device_id_type=MESH
        )

    loads = [
        pltpu.make_async_copy(wv_hbm.at[0], wv_s, load_sem.at[0]),
        pltpu.make_async_copy(wp_hbm.at[0], wp_s, load_sem.at[1]),
    ]
    for unit in range(units):
        part = pl.ds(unit * unit_rows, unit_rows)
        loads.append(pltpu.make_async_copy(x_hbm.at[unit], x_s.at[part], load_sem.at[2 + unit]))
    for unit in range(units):
        part = pl.ds(unit * unit_rows, unit_rows)
        loads.append(
            pltpu.make_async_copy(up_hbm.at[unit], up_s.at[part], load_sem.at[2 + units + unit])
        )
    for load in [loads[2], loads[0], loads[1]] + loads[3:]:
        load.start()

    total = guide_ref.shape[1]
    half = total // 2
    samples = bin_ref.shape[1]
    sample = (me * unit_rows) // (unit_rows * group // samples)
    lane = lax.broadcasted_iota(jnp.int32, (units, half), 1).astype(jnp.float32)
    frequency = jnp.exp(-math.log(10000.0) * lane / half)
    which = lax.broadcasted_iota(jnp.int32, (units, half), 0)
    times = jnp.zeros((units, half), jnp.float32)
    for unit in range(units):
        times = jnp.where(which == unit, time_ref[unit, sample].astype(jnp.float32), times)
    angle = times * frequency
    waves = jnp.concatenate([jnp.sin(angle), jnp.cos(angle)], axis=1)
    table = guide_ref[...].astype(jnp.float32)
    bins = lax.broadcasted_iota(jnp.int32, table.shape, 0)
    for unit in range(units):
        picked = jnp.sum(
            jnp.where(bins == bin_ref[unit, sample], table, 0.0), axis=0, keepdims=True
        )
        picked = picked + 0.5 * waves[unit:unit + 1]
        for index in range(3):
            lanes = slice(index * width, (index + 1) * width)
            rows_s[unit, index] = picked[:, lanes] + section_ref[0, index:index + 1]
    tab_s[...] = jnp.zeros_like(tab_s)

    def hop(index):
        part = pl.ds(pl.multiple_of(index * piece, piece), piece)
        return pltpu.make_async_remote_copy(
            src_ref=send_s.at[part],
            dst_ref=arrive_s.at[part],
            send_sem=hop_send.at[index],
            recv_sem=hop_recv.at[index],
            device_id={"section": 1 - section},
            device_id_type=MESH,
        )

    def each_chunk(start, size, body):
        @pl.loop(0, size // chunk)
        def step(index):
            body(pl.ds(pl.multiple_of(start + index * chunk, chunk), chunk), index * chunk)

    def multiply(size, body):
        tile = math.gcd(size, 768)

        @pl.loop(0, size // tile)
        def step(index):
            body(pl.ds(pl.multiple_of(index * tile, tile), tile))

    def add_rows(index, value):
        tab_s[index] += jnp.sum(value.reshape(chunk // 8, 8, width), axis=0)

    def forward(index, source, send):
        start = pl.multiple_of(index * piece, piece)
        unit = start // unit_rows
        rows = pl.ds(start, piece)

        def modulate(part, unused):
            normed, inverse = normalize(source[part].astype(jnp.float32))
            scaled = normed * (1.0 + rows_s[unit, 1]) + rows_s[unit, 0]
            mod_s[part] = scaled.astype(jnp.bfloat16)

        def first_dot(part):
            val_s[rows, part] = jnp.dot(
                mod_s[rows], wv_s[:, part], preferred_element_type=jnp.float32
            ).astype(jnp.bfloat16)

        def second_dot(part):
            proj_s[rows, part] = jnp.dot(
                val_s[rows], wp_s[:, part], preferred_element_type=jnp.float32
            )

        def add_gated(part, unused):
            hidden = source[part].astype(jnp.float32)
            block_out = hidden + rows_s[unit, 2] * proj_s[part]
            send_s[part] = block_out.astype(jnp.bfloat16)

        each_chunk(start, piece, modulate)
        multiply(depth, first_dot)
        multiply(width, second_dot)
        if send:
            each_chunk(start, piece, add_gated)

    def gated(index, upstream):
        start = pl.multiple_of(index * piece, piece)
        unit = start // unit_rows

        def body(part, unused):
            grad_up = upstream[part].astype(jnp.float32)
            right_s[0, part] = (rows_s[unit, 2] * grad_up).astype(jnp.bfloat16)
            add_rows(2, grad_up * proj_s[part])

        each_chunk(start, piece, body)

    def to_values(index):
        rows = pl.ds(pl.multiple_of(index * piece, piece), piece)

        def body(part):
            right_s[1, rows, part] = lax.dot_general(
                right_s[0, rows], wp_s[part, :], (((1,), (1,)), ((), ())),
                preferred_element_type=jnp.float32,
            ).astype(jnp.bfloat16)

        multiply(depth, body)

    def to_input(start, size, source, upstream):
        start = pl.multiple_of(start, size)
        unit = start // unit_rows
        rows = pl.ds(start, size)

        def dot(part):
            gm_s[pl.ds(0, size), part] = lax.dot_general(
                right_s[1, rows], wv_s[part, :], (((1,), (1,)), ((), ())),
                preferred_element_type=jnp.float32,
            )

        def body(part, offset):
            normed, inverse = normalize(source[part].astype(jnp.float32))
            grad_mod = gm_s[pl.ds(pl.multiple_of(offset, chunk), chunk)]
            add_rows(0, grad_mod)
            add_rows(1, grad_mod * normed)
            if upstream is not None:
                grad_norm = grad_mod * (1.0 + rows_s[unit, 1])
                centre_grad = jnp.mean(grad_norm, axis=-1, keepdims=True)
                cross = jnp.mean(grad_norm * normed, axis=-1, keepdims=True)
                grad_up = upstream[part].astype(jnp.float32)
                grad_in = grad_up + inverse * (grad_norm - centre_grad - normed * cross)
                send_s[part] = grad_in.astype(jnp.bfloat16)

        multiply(width, dot)
        each_chunk(start, size, body)

    def turn_left(unit):
        part = pl.ds(pl.multiple_of(unit * unit_rows, unit_rows), unit_rows)
        left_s[0, :, part] = val_s[part].T
        left_s[1, :, part] = mod_s[part].T

    @pl.when(section == 0)
    def earlier():
        for load in loads[2:2 + units]:
            load.wait()
        loads[0].wait()
        loads[1].wait()
        pl.semaphore_wait(barrier, group)

        @pl.loop(0, hops)
        def out(index):
            forward(index, x_s, True)
            hop(index).start()

        @pl.loop(0, units)
        def turn(unit):
            turn_left(unit)

        for load in loads[2 + units:]:
            load.wait()

        @pl.loop(0, hops)
        def back(index):
            hop(index).wait_recv()
            gated(index, arrive_s)
            to_values(index)

    @pl.when(section == 1)
    def later():
        for load in loads:
            load.wait()
        pl.semaphore_wait(barrier, group)

        @pl.loop(0, hops)
        def both(index):
            hop(index).wait_recv()
            forward(index, arrive_s, False)
            gated(index, up_s)
            to_values(index)
            to_input(index * piece, piece, arrive_s, up_s)
            hop(index).start()

        @pl.loop(0, units)
        def turn(unit):
            turn_left(unit)

    ranks = [sorted(range(far), key=lambda block: -abs(block - spot)) for spot in range(far)]
    order = [(0, rank) for rank in range(far - 1)] + [(1, rank) for rank in range(far - 1)]
    order = order + [(0, far - 1), (1, far - 1)]
    pieces = len(order)
    block_rows = left_s.shape[1] // group
    per_matrix = far - 1

    def chosen(values):
        result = 0
        for spot in range(far):
            away = (place - spot + far) % far
            result = result + values[spot] * (1 - (away + far - 1) // far)
        return result

    blocks = [chosen([ranks[spot][rank] for spot in range(far)]) for rank in range(far)]

    def partial(turn, index):
        matrix, rank = order[index]
        which = (1 - side) if turn == 0 else side
        first = pl.multiple_of((blocks[rank] * 2 + which) * 2 * block_rows, 2 * block_rows)
        product = jnp.dot(
            left_s[matrix, pl.ds(first, 2 * block_rows)], right_s[matrix],
            preferred_element_type=jnp.float32,
        ).astype(jnp.bfloat16)
        kept = side_out if turn == 0 else own_s

        @pl.when(core == 0)
        def even():
            kept[index] = product[:block_rows]
            core_out[turn, index] = product[block_rows:]

        @pl.when(core == 1)
        def odd():
            kept[index] = product[block_rows:]
            core_out[turn, index] = product[:block_rows]

    def core_copy(turn, index):
        return pltpu.make_async_remote_copy(
            src_ref=core_out.at[turn, index],
            dst_ref=core_in.at[turn, index],
            send_sem=core_send.at[turn, index],
            recv_sem=core_recv.at[turn, index],
            device_id={"dp": me + 1 - 2 * core},
            device_id_type=MESH,
        )

    def side_copy(index):
        return pltpu.make_async_remote_copy(
            src_ref=side_out.at[index],
            dst_ref=side_in.at[index],
            send_sem=side_send.at[index],
            recv_sem=side_recv.at[index],
            device_id={"dp": me + 2 - 4 * side},
            device_id_type=MESH,
        )

    def over_block(body):
        tall = math.gcd(block_rows, 16)

        @pl.loop(0, block_rows // tall)
        def step(at):
            body(pl.ds(pl.multiple_of(at * tall, tall), tall))

    def send_side(index):
        core_copy(0, index).wait_recv()

        def add(part):
            mine = side_out[index, part].astype(jnp.float32)
            mine = mine + core_in[0, index, part].astype(jnp.float32)
            side_out[index, part] = mine.astype(jnp.bfloat16)

        over_block(add)
        side_copy(index).start()

    for index in range(pieces):
        partial(0, index)
        core_copy(0, index).start()
        if index > 0:
            send_side(index - 1)
    for index in range(pieces):
        partial(1, index)
        core_copy(1, index).start()
        if index == 0:
            send_side(pieces - 1)

    def up_copy(matrix, block):
        return pltpu.make_async_remote_copy(
            src_ref=own_s.at[order.index((matrix, rank_of(block)))],
            dst_ref=low_in.at[matrix, block],
            send_sem=low_send.at[matrix, block],
            recv_sem=low_recv.at[matrix, block],
            device_id={"dp": (me + 4) % group},
            device_id_type=MESH,
        )

    def down_copy(matrix, block):
        return pltpu.make_async_remote_copy(
            src_ref=own_s.at[order.index((matrix, rank_of(block)))],
            dst_ref=high_in.at[matrix, block],
            send_sem=high_send.at[matrix, block],
            recv_sem=high_recv.at[matrix, block],
            device_id={"dp": (me + group - 4) % group},
            device_id_type=MESH,
        )

    spot_now = [0]

    def rank_of(block):
        return ranks[spot_now[0]].index(block)

    def chain(spot, indices):
        spot_now[0] = spot
        for index in indices:
            matrix, rank = order[index]
            block = ranks[spot][rank]
            core_copy(1, index).wait_recv()
            side_copy(index).wait_recv()
            terms = []
            if block >= spot and spot > 0:
                up_copy(matrix, block).wait_recv()
                terms.append(low_in)
            if block <= spot and spot < far - 1:
                down_copy(matrix, block).wait_recv()
                terms.append(high_in)

            def add(part):
                mine = own_s[index, part].astype(jnp.float32)
                mine = mine + core_in[1, index, part].astype(jnp.float32)
                mine = mine + side_in[index, part].astype(jnp.float32)
                for term in terms:
                    mine = mine + term[matrix, block, part].astype(jnp.float32)
                if block == spot:
                    (proj_out, value_out)[matrix][part] = mine
                else:
                    own_s[index, part] = mine.astype(jnp.bfloat16)

            over_block(add)
            if block > spot:
                up_copy(matrix, block).start()
            elif block < spot:
                down_copy(matrix, block).start()

    def finish(spot):
        spot_now[0] = spot
        for matrix in range(2):
            for block in range(far):
                if block > spot:
                    up_copy(matrix, block).wait_send()
                elif block < spot:
                    down_copy(matrix, block).wait_send()

    def stage(indices):
        for spot in range(far):
            @pl.when(place == spot)
            def run(spot=spot):
                chain(spot, indices)

    stage(range(0, 1))

    @pl.when(section == 0)
    def rest():
        @pl.loop(0, units)
        def one(unit):
            to_input(unit * unit_rows, unit_rows, x_s, None)

    lanes = table_out.shape[1]
    table = jnp.concatenate(
        [jnp.sum(tab_s[index], axis=0, keepdims=True) for index in range(3)]
        + [jnp.zeros((5, width), jnp.float32)], axis=0,
    )
    for owner in range(group):
        tables_s[owner, :, :lanes] = table[:, owner * lanes:(owner + 1) * lanes]

    def table_copy(step):
        return pltpu.make_async_remote_copy(
            src_ref=tables_s.at[(me + step) % group],
            dst_ref=tables_in.at[step - 1],
            send_sem=table_send.at[step - 1],
            recv_sem=table_recv.at[step - 1],
            device_id={"dp": (me + step) % group},
            device_id_type=MESH,
        )

    for step in range(1, group):
        table_copy(step).start()
    stage(range(1, pieces))
    sums = tables_s[me]
    for step in range(1, group):
        table_copy(step).wait_recv()
        sums = sums + tables_in[step - 1]
    table_out[...] = sums[:, :lanes]

    @pl.loop(0, hops)
    def sent(index):
        hop(index).wait_send()

    for index in range(pieces):
        core_copy(0, index).wait_send()
        core_copy(1, index).wait_send()
        side_copy(index).wait_send()
    for step in range(1, group):
        table_copy(step).wait_send()
    for spot in range(far):
        @pl.when(place == spot)
        def drain(spot=spot):
            finish(spot)


def per_device(
    inputs, out_grad, guide_bin, time_step, guide_table, section_table, value_weight, proj_weight
):
    units, rows, width = inputs.shape
    depth = value_weight.shape[2]
    group = lax.axis_size("dp")
    per_sample = rows * group // guide_bin.shape[1]
    if (lax.axis_size("section") != 2 or group % 4 or per_sample % rows or rows % 128
            or width != depth or width % (group * 16)):
        return per_device_scan(
            inputs, out_grad, guide_bin, time_step, guide_table, section_table,
            value_weight, proj_weight,
        )
    far = group // 4
    count = units * rows
    piece = PIECE_ROWS
    hops = count // piece
    block = (width // group, width)
    pieces = 2 * far
    lanes = width // group
    vmem = pl.BlockSpec(memory_space=pltpu.VMEM)
    smem = pl.BlockSpec(memory_space=pltpu.SMEM)
    hbm = pl.BlockSpec(memory_space=pl.ANY)
    dma = pltpu.SemaphoreType.DMA
    half = jnp.bfloat16
    value_sum, proj_sum, table_sum = pl.pallas_call(
        functools.partial(step_kernel, far),
        out_shape=(
            jax.ShapeDtypeStruct(block, jnp.float32),
            jax.ShapeDtypeStruct(block, jnp.float32),
            jax.ShapeDtypeStruct((8, lanes), jnp.float32),
        ),
        in_specs=[smem, smem, vmem, vmem, hbm, hbm, hbm, hbm],
        out_specs=(vmem,) * 3,
        scratch_shapes=[
            pltpu.VMEM((count, width), half),
            pltpu.VMEM((count, width), half),
            pltpu.VMEM((width, depth), half),
            pltpu.VMEM((depth, width), half),
            pltpu.VMEM((units, 3, 1, width), jnp.float32),
            pltpu.VMEM((count, width), half),
            pltpu.VMEM((count, width), half),
            pltpu.VMEM((count, width), half),
            pltpu.VMEM((count, depth), half),
            pltpu.VMEM((2, width, count), half),
            pltpu.VMEM((2, count, width), half),
            pltpu.VMEM((count, width), jnp.float32),
            pltpu.VMEM((rows, width), jnp.float32),
            pltpu.VMEM((3, 8, width), jnp.float32),
            pltpu.VMEM((2, pieces) + block, half),
            pltpu.VMEM((2, pieces) + block, half),
            pltpu.VMEM((pieces,) + block, half),
            pltpu.VMEM((pieces,) + block, half),
            pltpu.VMEM((pieces,) + block, half),
            pltpu.VMEM((2, far) + block, half),
            pltpu.VMEM((2, far) + block, half),
            pltpu.VMEM((group, 8, 128), jnp.float32),
            pltpu.VMEM((group - 1, 8, 128), jnp.float32),
            dma((2 + 2 * units,)), dma((hops,)), dma((hops,)), dma((2, pieces)), dma((2, pieces)),
            dma((pieces,)), dma((pieces,)), dma((2, far)), dma((2, far)), dma((2, far)),
            dma((2, far)), dma((group - 1,)), dma((group - 1,)),
        ],
        compiler_params=pltpu.CompilerParams(
            collective_id=0, has_side_effects=True, vmem_limit_bytes=62 * 1024 * 1024
        ),
    )(
        guide_bin, time_step, guide_table, section_table, inputs, out_grad,
        value_weight, proj_weight,
    )
    return (value_sum[None], proj_sum[None], table_sum[None, :3])


def solution(mesh):
    return jax.shard_map(
        per_device,
        mesh=mesh,
        in_specs=(
            P(None, "dp", None),
            P(None, "dp", None),
            P(),
            P(),
            P(),
            P("section", None, None),
            P("section", None, None),
            P("section", None, None),
        ),
        out_specs=(P("section", "dp", None), P("section", "dp", None), P("section", None, "dp")),
        check_vma=False,
    )
```

time: 165 us -> 147 us (0.89)
  matrix products: 11.2 us -> 0 us
  Pallas kernels: 143 us -> 137 us
  other arithmetic: 4.77 us -> 0 us
  local copies, waits for them, and re-layouts: 5.52 us -> 9.02 us
    dot_general x2 -> x0, matrix products: 11.2 us -> none  [contract_rows(): lax.dot_general(left, right, (((0,), (0,)), ((), ())), preferred_element_...]
    pallas_call x2 -> x1, Pallas kernels: 143 us -> 137 us  [per_device(): pl.pallas_call(functools.partial(step_kernel, far), out_shape=(jax.ShapeD...]
    unnamed x10 -> x6, local copies, waits for them, and re-layouts: 4.04 us -> 8.34 us
where the time goes in v1:
time: 147 us
  Pallas kernels  137 us (93%)
  local copies, waits for them, and re-layouts  9.02 us (6%)
    pallas_call x1, Pallas kernels, per_device(): pl.pallas_call(functools.partial(step_kernel, far), out_shape=(jax.ShapeD...  137 us
    unnamed x6, local copies, waits for them, and re-layouts  8.34 us

profile of v1, /device:TPU:0, one launch (start us, length us, event | category | flops | bytes accessed | tf_op | source)
XLA Modules:
  0.0 147.1 jit_solution(11579369726785602100)
XLA Ops:
  0.6 1.3 copy.11.bin_ref
  1.9 1.3 copy.12.time_ref
  3.2 1.3 copy.13.section_ref
  4.6 137.5 %shard_map.103 = (f32[96,1536]{1,0:T(8,128)}, f32[96,1536]{1,0:T(8,128)}, f32[8,96]{1,0:T(8,128)}) custom-call(s32[4,1]{1,0:T(4,128)} %copy.11.bin_ref, s32[4,1]{1,0:T(4,128)} %copy.12.time_ref, bf16[32,4608]{1,0:T(8,128)(2,1)} %guide_ref.1, f32[1,3,1536]{2,1,0:T(4,128)} %copy.13.section_ref, bf16[4,128,1536]{2,1,0:T(8,128)(2,1)} %x_hbm.1, ...), custom_call_target="tpu_custom_call" | custom-call | tf_op jit(solution)/shard_map/pallas_call | solution.py:693
  142.0 0.7 slice_bitcast_fusion
  142.7 0.6 copy.14
  143.3 1.9 %copy.17 = f32[1,96,1536]{2,1,0:T(8,128)} copy(f32[1,96,1536]{2,1,0:T(8,128)} %bitcast.5) | data formatting | bytes 1179648
  145.2 1.9 %copy.18 = f32[1,96,1536]{2,1,0:T(8,128)} copy(f32[1,96,1536]{2,1,0:T(8,128)} %bitcast.4) | data formatting | bytes 1179648

commit v2 on v1

--- a/solution.py
+++ b/solution.py
@@ -9,7 +9,11 @@
 from jax.sharding import PartitionSpec as P
 
 NORM_FLOOR = 0.1
-PIECE_ROWS = 64
+PIECE_ROWS = 32
+FORWARD_ROWS = 64
+CHUNK_ROWS = 16
+UNROLL = 2
+TILE = 1536
 
 
 def shifted(value, axis, steps):
@@ -237,17 +241,17 @@
 
 def step_kernel(far, bin_ref, time_ref, guide_ref, section_ref, x_hbm, up_hbm, wv_hbm, wp_hbm,
                 value_out, proj_out, table_out,
-                x_s, up_s, wv_s, wp_s, rows_s, arrive_s, send_s, mod_s, val_s, left_s, right_s,
-                proj_s, gm_s, tab_s, core_out, core_in, own_s, side_out, side_in, low_in, high_in,
+                local_s, wv_s, wp_s, rows_s, arrive_s, send_s, mod_s, val_s, left_s, right_s,
+                wide_s, part_s, tab_s, core_out, core_in, own_s, side_out, side_in, low_in, high_in,
                 tables_s, tables_in, load_sem, hop_send, hop_recv, core_send, core_recv,
                 side_send, side_recv, low_send, low_recv, high_send, high_recv,
                 table_send, table_recv):
     units, unit_rows = x_hbm.shape[0], x_hbm.shape[1]
-    count, width = x_s.shape
+    count, width = local_s.shape
     depth = wv_s.shape[1]
     hops = hop_send.shape[0]
     piece = count // hops
-    chunk = math.gcd(piece, 32)
+    per_unit = unit_rows // piece
     group = 4 * far
     section = lax.axis_index("section")
     me = lax.axis_index("dp")
@@ -262,43 +266,53 @@
             barrier, inc=1, device_id={"dp": (me + step) % group}, device_id_type=MESH
         )
 
-    loads = [
-        pltpu.make_async_copy(wv_hbm.at[0], wv_s, load_sem.at[0]),
-        pltpu.make_async_copy(wp_hbm.at[0], wp_s, load_sem.at[1]),
-    ]
-    for unit in range(units):
+    def load_rows(source, unit):
         part = pl.ds(unit * unit_rows, unit_rows)
-        loads.append(pltpu.make_async_copy(x_hbm.at[unit], x_s.at[part], load_sem.at[2 + unit]))
-    for unit in range(units):
-        part = pl.ds(unit * unit_rows, unit_rows)
-        loads.append(
-            pltpu.make_async_copy(up_hbm.at[unit], up_s.at[part], load_sem.at[2 + units + unit])
-        )
-    for load in [loads[2], loads[0], loads[1]] + loads[3:]:
-        load.start()
+        return pltpu.make_async_copy(source.at[unit], local_s.at[part], load_sem.at[2 + unit])
+
+    load_value = pltpu.make_async_copy(wv_hbm.at[0], wv_s, load_sem.at[0])
+    load_proj = pltpu.make_async_copy(wp_hbm.at[0], wp_s, load_sem.at[1])
+
+    @pl.when(section == 0)
+    def load_first():
+        load_rows(x_hbm, 0).start()
+        load_value.start()
+        load_proj.start()
+        for unit in range(1, units):
+            load_rows(x_hbm, unit).start()
+
+    @pl.when(section == 1)
+    def load_last():
+        load_rows(up_hbm, 0).start()
+        load_proj.start()
+        load_value.start()
+        for unit in range(1, units):
+            load_rows(up_hbm, unit).start()
 
     total = guide_ref.shape[1]
     half = total // 2
-    samples = bin_ref.shape[1]
+    samples = bin_ref.shape[0] // units
     sample = (me * unit_rows) // (unit_rows * group // samples)
     lane = lax.broadcasted_iota(jnp.int32, (units, half), 1).astype(jnp.float32)
     frequency = jnp.exp(-math.log(10000.0) * lane / half)
     which = lax.broadcasted_iota(jnp.int32, (units, half), 0)
     times = jnp.zeros((units, half), jnp.float32)
     for unit in range(units):
-        times = jnp.where(which == unit, time_ref[unit, sample].astype(jnp.float32), times)
+        time = time_ref[unit * samples + sample].astype(jnp.float32)
+        times = jnp.where(which == unit, time, times)
     angle = times * frequency
     waves = jnp.concatenate([jnp.sin(angle), jnp.cos(angle)], axis=1)
     table = guide_ref[...].astype(jnp.float32)
     bins = lax.broadcasted_iota(jnp.int32, table.shape, 0)
     for unit in range(units):
         picked = jnp.sum(
-            jnp.where(bins == bin_ref[unit, sample], table, 0.0), axis=0, keepdims=True
+            jnp.where(bins == bin_ref[unit * samples + sample], table, 0.0),
+            axis=0, keepdims=True,
         )
         picked = picked + 0.5 * waves[unit:unit + 1]
         for index in range(3):
             lanes = slice(index * width, (index + 1) * width)
-            rows_s[unit, index] = picked[:, lanes] + section_ref[0, index:index + 1]
+            rows_s[unit, index] = picked[:, lanes] + section_ref[index]
     tab_s[...] = jnp.zeros_like(tab_s)
 
     def hop(index):
@@ -313,65 +327,32 @@
         )
 
     def each_chunk(start, size, body):
-        @pl.loop(0, size // chunk)
+        tall = math.gcd(size, CHUNK_ROWS)
+
+        @pl.loop(0, size // tall, unroll=min(UNROLL, size // tall))
         def step(index):
-            body(pl.ds(pl.multiple_of(start + index * chunk, chunk), chunk), index * chunk)
+            body(pl.ds(pl.multiple_of(start + index * tall, tall), tall), index * tall)
 
     def multiply(size, body):
-        tile = math.gcd(size, 768)
+        tile = math.gcd(size, TILE)
 
         @pl.loop(0, size // tile)
         def step(index):
             body(pl.ds(pl.multiple_of(index * tile, tile), tile))
 
     def add_rows(index, value):
-        tab_s[index] += jnp.sum(value.reshape(chunk // 8, 8, width), axis=0)
-
-    def forward(index, source, send):
-        start = pl.multiple_of(index * piece, piece)
-        unit = start // unit_rows
-        rows = pl.ds(start, piece)
-
-        def modulate(part, unused):
-            normed, inverse = normalize(source[part].astype(jnp.float32))
-            scaled = normed * (1.0 + rows_s[unit, 1]) + rows_s[unit, 0]
-            mod_s[part] = scaled.astype(jnp.bfloat16)
-
-        def first_dot(part):
-            val_s[rows, part] = jnp.dot(
-                mod_s[rows], wv_s[:, part], preferred_element_type=jnp.float32
-            ).astype(jnp.bfloat16)
-
-        def second_dot(part):
-            proj_s[rows, part] = jnp.dot(
-                val_s[rows], wp_s[:, part], preferred_element_type=jnp.float32
-            )
-
-        def add_gated(part, unused):
-            hidden = source[part].astype(jnp.float32)
-            block_out = hidden + rows_s[unit, 2] * proj_s[part]
-            send_s[part] = block_out.astype(jnp.bfloat16)
-
-        each_chunk(start, piece, modulate)
-        multiply(depth, first_dot)
-        multiply(width, second_dot)
-        if send:
-            each_chunk(start, piece, add_gated)
-
-    def gated(index, upstream):
-        start = pl.multiple_of(index * piece, piece)
-        unit = start // unit_rows
-
-        def body(part, unused):
-            grad_up = upstream[part].astype(jnp.float32)
-            right_s[0, part] = (rows_s[unit, 2] * grad_up).astype(jnp.bfloat16)
-            add_rows(2, grad_up * proj_s[part])
-
-        each_chunk(start, piece, body)
-
-    def to_values(index):
-        rows = pl.ds(pl.multiple_of(index * piece, piece), piece)
-
+        rows = value.shape[0]
+        tab_s[index] += jnp.sum(value.reshape(rows // 8, 8, width), axis=0)
+
+    def to_depth(rows, part):
+        val_s[rows, part] = jnp.dot(
+            mod_s[rows], wv_s[:, part], preferred_element_type=jnp.float32
+        ).astype(jnp.bfloat16)
+
+    def to_width(rows, part):
+        return jnp.dot(val_s[rows], wp_s[:, part], preferred_element_type=jnp.float32)
+
+    def to_values(rows):
         def body(part):
             right_s[1, rows, part] = lax.dot_general(
                 right_s[0, rows], wp_s[part, :], (((1,), (1,)), ((), ())),
@@ -380,78 +361,183 @@
 
         multiply(depth, body)
 
-    def to_input(start, size, source, upstream):
-        start = pl.multiple_of(start, size)
-        unit = start // unit_rows
-        rows = pl.ds(start, size)
-
-        def dot(part):
-            gm_s[pl.ds(0, size), part] = lax.dot_general(
+    def to_mod(rows, target, target_rows):
+        def body(part):
+            target[target_rows, part] = lax.dot_general(
                 right_s[1, rows], wv_s[part, :], (((1,), (1,)), ((), ())),
                 preferred_element_type=jnp.float32,
             )
 
+        multiply(width, body)
+
+    def unit_rows_at(unit):
+        return pl.ds(pl.multiple_of(unit * unit_rows, unit_rows), unit_rows)
+
+    def turn_left(unit):
+        part = unit_rows_at(unit)
+        left_s[0, :, part] = val_s[part].T
+        left_s[1, :, part] = mod_s[part].T
+
+    def forward(index, size):
+        start = pl.multiple_of(index * size, size)
+        unit = start // unit_rows
+        rows = pl.ds(start, size)
+
+        def modulate(part, unused):
+            normed, inverse = normalize(local_s[part].astype(jnp.float32))
+            scaled = normed * (1.0 + rows_s[unit, 1]) + rows_s[unit, 0]
+            mod_s[part] = scaled.astype(jnp.bfloat16)
+
+        each_chunk(start, size, modulate)
+        multiply(depth, lambda part: to_depth(rows, part))
+
+        def second(part):
+            wide_s[rows, part] = to_width(rows, part)
+
+        multiply(width, second)
+
+        def add_gated(part, unused):
+            hidden = local_s[part].astype(jnp.float32)
+            block_out = hidden + rows_s[unit, 2] * wide_s[part]
+            send_s[part] = block_out.astype(jnp.bfloat16)
+
+        for at in range(size // piece):
+            each_chunk(start + at * piece, piece, add_gated)
+            hop(index * (size // piece) + at).start()
+
+    def receive(index):
+        start = pl.multiple_of(index * piece, piece)
+        unit = start // unit_rows
+        hop(index).wait_recv()
+
+        def body(part, unused):
+            grad_up = arrive_s[part].astype(jnp.float32)
+            right_s[0, part] = (rows_s[unit, 2] * grad_up).astype(jnp.bfloat16)
+            add_rows(2, grad_up * wide_s[part])
+
+        each_chunk(start, piece, body)
+
+    def table_rows(unit):
+        to_mod(unit_rows_at(unit), part_s, slice(None))
+
         def body(part, offset):
-            normed, inverse = normalize(source[part].astype(jnp.float32))
-            grad_mod = gm_s[pl.ds(pl.multiple_of(offset, chunk), chunk)]
+            normed, inverse = normalize(local_s[part].astype(jnp.float32))
+            grad_mod = part_s[pl.ds(offset, part.size)]
             add_rows(0, grad_mod)
             add_rows(1, grad_mod * normed)
-            if upstream is not None:
-                grad_norm = grad_mod * (1.0 + rows_s[unit, 1])
-                centre_grad = jnp.mean(grad_norm, axis=-1, keepdims=True)
-                cross = jnp.mean(grad_norm * normed, axis=-1, keepdims=True)
-                grad_up = upstream[part].astype(jnp.float32)
-                grad_in = grad_up + inverse * (grad_norm - centre_grad - normed * cross)
-                send_s[part] = grad_in.astype(jnp.bfloat16)
-
-        multiply(width, dot)
-        each_chunk(start, size, body)
-
-    def turn_left(unit):
-        part = pl.ds(pl.multiple_of(unit * unit_rows, unit_rows), unit_rows)
-        left_s[0, :, part] = val_s[part].T
-        left_s[1, :, part] = mod_s[part].T
+
+        each_chunk(unit * unit_rows, unit_rows, body)
 
     @pl.when(section == 0)
     def earlier():
-        for load in loads[2:2 + units]:
-            load.wait()
-        loads[0].wait()
-        loads[1].wait()
+        load_rows(x_hbm, 0).wait()
+        load_value.wait()
+        load_proj.wait()
+        for unit in range(1, units):
+            load_rows(x_hbm, unit).wait()
         pl.semaphore_wait(barrier, group)
-
-        @pl.loop(0, hops)
+        size = math.gcd(unit_rows, FORWARD_ROWS)
+
+        @pl.loop(0, count // size)
         def out(index):
-            forward(index, x_s, True)
-            hop(index).start()
+            forward(index, size)
 
         @pl.loop(0, units)
-        def turn(unit):
+        def back(unit):
             turn_left(unit)
 
-        for load in loads[2 + units:]:
-            load.wait()
-
-        @pl.loop(0, hops)
-        def back(index):
-            hop(index).wait_recv()
-            gated(index, arrive_s)
-            to_values(index)
+            @pl.loop(0, per_unit)
+            def one(at):
+                receive(unit * per_unit + at)
+
+            to_values(unit_rows_at(unit))
+
+    def grads_ahead(unit):
+        def body(part, unused):
+            grad_up = local_s[part].astype(jnp.float32)
+            right_s[0, part] = (rows_s[unit, 2] * grad_up).astype(jnp.bfloat16)
+
+        each_chunk(unit * unit_rows, unit_rows, body)
+        to_values(unit_rows_at(unit))
+
+    def mods_ahead(unit):
+        rows = unit_rows_at(unit)
+        to_mod(rows, wide_s, rows)
+
+    def values_behind(unit):
+        multiply(depth, lambda part: to_depth(unit_rows_at(unit), part))
+
+    def gates_behind(unit):
+        rows = unit_rows_at(unit)
+
+        def second(part):
+            part_s[:, part] = to_width(rows, part)
+
+        multiply(width, second)
+
+        def body(part, offset):
+            add_rows(2, local_s[part].astype(jnp.float32) * part_s[pl.ds(offset, part.size)])
+
+        each_chunk(unit * unit_rows, unit_rows, body)
+
+    def answer(index):
+        start = pl.multiple_of(index * piece, piece)
+        unit = start // unit_rows
+        hop(index).wait_recv()
+
+        def body(part, unused):
+            normed, inverse = normalize(arrive_s[part].astype(jnp.float32))
+            scale = 1.0 + rows_s[unit, 1]
+            mod_s[part] = (normed * scale + rows_s[unit, 0]).astype(jnp.bfloat16)
+            grad_mod = wide_s[part]
+            add_rows(0, grad_mod)
+            add_rows(1, grad_mod * normed)
+            grad_norm = grad_mod * scale
+            centre_grad = jnp.mean(grad_norm, axis=-1, keepdims=True)
+            cross = jnp.mean(grad_norm * normed, axis=-1, keepdims=True)
+            grad_up = local_s[part].astype(jnp.float32)
+            grad_in = grad_up + inverse * (grad_norm - centre_grad - normed * cross)
+            send_s[part] = grad_in.astype(jnp.bfloat16)
+
+        each_chunk(start, piece, body)
+        hop(index).start()
 
     @pl.when(section == 1)
     def later():
-        for load in loads:
-            load.wait()
+        load_rows(up_hbm, 0).wait()
+        load_proj.wait()
+        load_value.wait()
+        for unit in range(1, units):
+            load_rows(up_hbm, unit).wait()
+        for unit in range(min(2, units)):
+            grads_ahead(unit)
+            mods_ahead(unit)
         pl.semaphore_wait(barrier, group)
 
-        @pl.loop(0, hops)
-        def both(index):
-            hop(index).wait_recv()
-            forward(index, arrive_s, False)
-            gated(index, up_s)
-            to_values(index)
-            to_input(index * piece, piece, arrive_s, up_s)
-            hop(index).start()
+        @pl.loop(0, units)
+        def both(unit):
+            @pl.loop(0, per_unit)
+            def one(at):
+                answer(unit * per_unit + at)
+
+                @pl.when((at == 0) & (unit + 2 < units))
+                def job_grads():
+                    grads_ahead(unit + 2)
+
+                @pl.when((at == 1) & (unit + 2 < units))
+                def job_mods():
+                    mods_ahead(unit + 2)
+
+                @pl.when((at == 2 % per_unit) & (unit >= 1))
+                def job_values():
+                    values_behind(unit - 1)
+
+                @pl.when((at == 3 % per_unit) & (unit >= 1))
+                def job_gates():
+                    gates_behind(unit - 1)
+
+        values_behind(units - 1)
+        gates_behind(units - 1)
 
         @pl.loop(0, units)
         def turn(unit):
@@ -614,15 +700,16 @@
             def run(spot=spot):
                 chain(spot, indices)
 
-    stage(range(0, 1))
-
-    @pl.when(section == 0)
-    def rest():
-        @pl.loop(0, units)
-        def one(unit):
-            to_input(unit * unit_rows, unit_rows, x_s, None)
-
-    lanes = table_out.shape[1]
+    ahead = min(units, pieces - 1)
+    for index in range(ahead):
+        stage([index])
+
+        @pl.when(section == 0)
+        def tables(index=index):
+            for unit in range(index, units if index == ahead - 1 else index + 1):
+                table_rows(unit)
+
+    lanes = table_out.shape[2]
     table = jnp.concatenate(
         [jnp.sum(tab_s[index], axis=0, keepdims=True) for index in range(3)]
         + [jnp.zeros((5, width), jnp.float32)], axis=0,
@@ -642,12 +729,13 @@
 
     for step in range(1, group):
         table_copy(step).start()
-    stage(range(1, pieces))
+    stage(range(ahead, pieces))
     sums = tables_s[me]
     for step in range(1, group):
         table_copy(step).wait_recv()
         sums = sums + tables_in[step - 1]
-    table_out[...] = sums[:, :lanes]
+    for index in range(3):
+        table_out[index] = sums[index:index + 1, :lanes]
 
     @pl.loop(0, hops)
     def sent(index):
@@ -680,7 +768,7 @@
         )
     far = group // 4
     count = units * rows
-    piece = PIECE_ROWS
+    piece = math.gcd(rows, PIECE_ROWS)
     hops = count // piece
     block = (width // group, width)
     pieces = 2 * far
@@ -695,12 +783,11 @@
         out_shape=(
             jax.ShapeDtypeStruct(block, jnp.float32),
             jax.ShapeDtypeStruct(block, jnp.float32),
-            jax.ShapeDtypeStruct((8, lanes), jnp.float32),
+            jax.ShapeDtypeStruct((3, 1, lanes), jnp.float32),
         ),
         in_specs=[smem, smem, vmem, vmem, hbm, hbm, hbm, hbm],
         out_specs=(vmem,) * 3,
         scratch_shapes=[
-            pltpu.VMEM((count, width), half),
             pltpu.VMEM((count, width), half),
             pltpu.VMEM((width, depth), half),
             pltpu.VMEM((depth, width), half),
@@ -723,7 +810,7 @@
             pltpu.VMEM((2, far) + block, half),
             pltpu.VMEM((group, 8, 128), jnp.float32),
             pltpu.VMEM((group - 1, 8, 128), jnp.float32),
-            dma((2 + 2 * units,)), dma((hops,)), dma((hops,)), dma((2, pieces)), dma((2, pieces)),
+            dma((2 + units,)), dma((hops,)), dma((hops,)), dma((2, pieces)), dma((2, pieces)),
             dma((pieces,)), dma((pieces,)), dma((2, far)), dma((2, far)), dma((2, far)),
             dma((2, far)), dma((group - 1,)), dma((group - 1,)),
         ],
@@ -731,10 +818,11 @@
             collective_id=0, has_side_effects=True, vmem_limit_bytes=62 * 1024 * 1024
         ),
     )(
-        guide_bin, time_step, guide_table, section_table, inputs, out_grad,
+        guide_bin.reshape(-1), time_step.reshape(-1), guide_table,
+        section_table.transpose(1, 0, 2), inputs, out_grad,
         value_weight, proj_weight,
     )
-    return (value_sum[None], proj_sum[None], table_sum[None, :3])
+    return (value_sum[None], proj_sum[None], table_sum.transpose(1, 0, 2))
 
 
 def solution(mesh):

time: 147 us -> 115 us (0.78)
  Pallas kernels: 137 us -> 109 us
  local copies, waits for them, and re-layouts: 9.02 us -> 5.05 us
    pallas_call x1, Pallas kernels: 137 us -> 109 us  [per_device(): pl.pallas_call(functools.partial(step_kernel, far), out_shape=(jax.ShapeD...]
    unnamed x6 -> x3, local copies, waits for them, and re-layouts: 8.34 us -> 5.05 us
where the time goes in v2:
time: 115 us
  Pallas kernels  109 us (95%)
  local copies, waits for them, and re-layouts  5.05 us (4%)
    pallas_call x1, Pallas kernels, per_device(): pl.pallas_call(functools.partial(step_kernel, far), out_shape=(jax.ShapeD...  109 us
    unnamed x3, local copies, waits for them, and re-layouts  5.05 us

profile of v2, /device:TPU:0, one launch (start us, length us, event | category | flops | bytes accessed | tf_op | source)
XLA Modules:
  0.0 114.8 jit_solution(6560405253619689971)
XLA Ops:
  0.6 109.2 %shard_map.103 = (f32[96,1536]{1,0:T(8,128)}, f32[96,1536]{1,0:T(8,128)}, f32[3,1,96]{2,1,0:T(1,128)}) custom-call(s32[4]{0:T(128)} %bitcast.10, s32[4]{0:T(128)} %bitcast.11, bf16[32,4608]{1,0:T(8,128)(2,1)} %guide_ref.1, f32[3,1,1536]{2,1,0:T(1,128)} %bitcast.8, bf16[4,128,1536]{2,1,0:T(8,128)(2,1)} %x_hbm.1, bf16[4,128,1536]{2,1,0:T(8,128)(2,1)} %up_hbm.1, ...), custom_call_target="tpu_custom_call" | custom-call | tf_op jit(solution)/shard_map/pallas_call | solution.py:781
  109.8 1.9 %copy.14 = f32[1,96,1536]{2,1,0:T(8,128)} copy(f32[1,96,1536]{2,1,0:T(8,128)} %bitcast.7) | data formatting | bytes 1179648
  111.7 1.9 %copy.15 = f32[1,96,1536]{2,1,0:T(8,128)} copy(f32[1,96,1536]{2,1,0:T(8,128)} %bitcast.6) | data formatting | bytes 1179648
  113.6 1.2 %copy.16 = f32[1,3,96]{2,0,1:T(1,128)} copy(f32[1,3,96]{2,0,1:T(1,128)} %bitcast.9) | data formatting | bytes 2304

commit v3 on v2

--- a/solution.py
+++ b/solution.py
@@ -14,6 +14,7 @@
 CHUNK_ROWS = 16
 UNROLL = 2
 TILE = 1536
+OWN_DEEP = 2
 
 
 def shifted(value, axis, steps):
@@ -242,9 +243,11 @@
 def step_kernel(far, bin_ref, time_ref, guide_ref, section_ref, x_hbm, up_hbm, wv_hbm, wp_hbm,
                 value_out, proj_out, table_out,
                 local_s, wv_s, wp_s, rows_s, arrive_s, send_s, mod_s, val_s, left_s, right_s,
-                wide_s, part_s, tab_s, core_out, core_in, own_s, side_out, side_in, low_in, high_in,
+                wide_s, part_s, tab_s, core_out, core_in, kept_s, side_out, side_in, low_in, high_in,
+                deep_s, deep_low, deep_high, cross_out, cross_in,
                 tables_s, tables_in, load_sem, hop_send, hop_recv, core_send, core_recv,
                 side_send, side_recv, low_send, low_recv, high_send, high_recv,
+                down_send, down_recv, rise_send, rise_recv, cross_send, cross_recv,
                 table_send, table_recv):
     units, unit_rows = x_hbm.shape[0], x_hbm.shape[1]
     count, width = local_s.shape
@@ -391,10 +394,20 @@
         each_chunk(start, size, modulate)
         multiply(depth, lambda part: to_depth(rows, part))
 
+        @pl.when(index == 0)
+        def load_second():
+            load_proj.wait()
+
         def second(part):
             wide_s[rows, part] = to_width(rows, part)
 
         multiply(width, second)
+
+        @pl.when(index == 0)
+        def enter():
+            for unit in range(1, units):
+                load_rows(x_hbm, unit).wait()
+            pl.semaphore_wait(barrier, group)
 
         def add_gated(part, unused):
             hidden = local_s[part].astype(jnp.float32)
@@ -432,10 +445,6 @@
     def earlier():
         load_rows(x_hbm, 0).wait()
         load_value.wait()
-        load_proj.wait()
-        for unit in range(1, units):
-            load_rows(x_hbm, unit).wait()
-        pl.semaphore_wait(barrier, group)
         size = math.gcd(unit_rows, FORWARD_ROWS)
 
         @pl.loop(0, count // size)
@@ -450,7 +459,9 @@
             def one(at):
                 receive(unit * per_unit + at)
 
-            to_values(unit_rows_at(unit))
+            @pl.when(unit < units - 1)
+            def values_now():
+                to_values(unit_rows_at(unit))
 
     def grads_ahead(unit):
         def body(part, unused):
@@ -567,16 +578,15 @@
             left_s[matrix, pl.ds(first, 2 * block_rows)], right_s[matrix],
             preferred_element_type=jnp.float32,
         ).astype(jnp.bfloat16)
-        kept = side_out if turn == 0 else own_s
 
         @pl.when(core == 0)
         def even():
-            kept[index] = product[:block_rows]
+            kept_s[turn, index] = product[:block_rows]
             core_out[turn, index] = product[block_rows:]
 
         @pl.when(core == 1)
         def odd():
-            kept[index] = product[block_rows:]
+            kept_s[turn, index] = product[block_rows:]
             core_out[turn, index] = product[:block_rows]
 
     def core_copy(turn, index):
@@ -606,84 +616,165 @@
         def step(at):
             body(pl.ds(pl.multiple_of(at * tall, tall), tall))
 
+    near = side_out.shape[2]
+    near_lanes, deep_lanes = slice(0, near), slice(near, width)
+    spot_now = [0]
+
+    def rank_of(block):
+        return ranks[spot_now[0]].index(block)
+
+    def row_copy(source, target, send_sem, recv_sem, matrix, block, away):
+        return pltpu.make_async_remote_copy(
+            src_ref=source.at[order.index((matrix, rank_of(block)))],
+            dst_ref=target.at[matrix, block],
+            send_sem=send_sem.at[matrix, block],
+            recv_sem=recv_sem.at[matrix, block],
+            device_id={"dp": (me + group + 4 * away) % group},
+            device_id_type=MESH,
+        )
+
+    def up_copy(matrix, block):
+        return row_copy(side_out, low_in, low_send, low_recv, matrix, block, 1)
+
+    def down_copy(matrix, block):
+        return row_copy(side_out, high_in, high_send, high_recv, matrix, block, -1)
+
+    def deep_up(matrix, block):
+        return row_copy(deep_s, deep_low, rise_send, rise_recv, matrix, block, 1)
+
+    def deep_down(matrix, block):
+        return row_copy(deep_s, deep_high, down_send, down_recv, matrix, block, -1)
+
+    def cross_copy(matrix):
+        return pltpu.make_async_remote_copy(
+            src_ref=cross_out.at[matrix],
+            dst_ref=cross_in.at[matrix],
+            send_sem=cross_send.at[matrix],
+            recv_sem=cross_recv.at[matrix],
+            device_id={"dp": me + 2 - 4 * side},
+            device_id_type=MESH,
+        )
+
+    outs = (proj_out, value_out)
+
+    def core_sum(turn, index, part, lanes):
+        mine = kept_s[turn, index, part, lanes].astype(jnp.float32)
+        return mine + core_in[turn, index, part, lanes].astype(jnp.float32)
+
     def send_side(index):
         core_copy(0, index).wait_recv()
 
         def add(part):
-            mine = side_out[index, part].astype(jnp.float32)
-            mine = mine + core_in[0, index, part].astype(jnp.float32)
-            side_out[index, part] = mine.astype(jnp.bfloat16)
+            side_out[index, part] = core_sum(0, index, part, near_lanes).astype(jnp.bfloat16)
+            deep_s[index, 0, part] = core_sum(0, index, part, deep_lanes).astype(jnp.bfloat16)
 
         over_block(add)
         side_copy(index).start()
+        core_copy(1, index).wait_recv()
+
+        def add_own(part):
+            deep_s[index, 1, part] = core_sum(1, index, part, deep_lanes).astype(jnp.bfloat16)
+
+        over_block(add_own)
+
+    def terms_of(spot, matrix, block, up, down, low, high):
+        terms = []
+        if block >= spot and spot > 0:
+            up(matrix, block).wait_recv()
+            terms.append(low)
+        if block <= spot and spot < far - 1:
+            down(matrix, block).wait_recv()
+            terms.append(high)
+        return terms
+
+    def deep_chain(spot, index):
+        spot_now[0] = spot
+        matrix, rank = order[index]
+        block = ranks[spot][rank]
+        terms = terms_of(spot, matrix, block, deep_up, deep_down, deep_low, deep_high)
+
+        def add(part):
+            for which in range(2):
+                mine = deep_s[index, which, part].astype(jnp.float32)
+                for term in terms:
+                    mine = mine + term[matrix, block, which, part].astype(jnp.float32)
+                if block != spot:
+                    deep_s[index, which, part] = mine.astype(jnp.bfloat16)
+                elif which == 0:
+                    cross_out[matrix, part] = mine.astype(jnp.bfloat16)
+                else:
+                    outs[matrix][part, deep_lanes] = mine
+
+        if terms or block == spot:
+            over_block(add)
+        if block > spot:
+            deep_up(matrix, block).start()
+        elif block < spot:
+            deep_down(matrix, block).start()
+        else:
+            cross_copy(matrix).start()
+
+    def chain(spot, index):
+        spot_now[0] = spot
+        matrix, rank = order[index]
+        block = ranks[spot][rank]
+        side_copy(index).wait_send()
+        side_copy(index).wait_recv()
+        terms = terms_of(spot, matrix, block, up_copy, down_copy, low_in, high_in)
+
+        def add(part):
+            mine = core_sum(1, index, part, near_lanes)
+            mine = mine + side_in[index, part].astype(jnp.float32)
+            for term in terms:
+                mine = mine + term[matrix, block, part].astype(jnp.float32)
+            if block == spot:
+                outs[matrix][part, near_lanes] = mine
+            else:
+                side_out[index, part] = mine.astype(jnp.bfloat16)
+
+        over_block(add)
+        if block > spot:
+            up_copy(matrix, block).start()
+        elif block < spot:
+            down_copy(matrix, block).start()
+
+    def at_spots(spots, body):
+        for spot in spots:
+            @pl.when(place == spot)
+            def run(spot=spot):
+                body(spot)
+
+    ends = sorted({0, far - 1})
+
+    def early(index):
+        send_side(index)
+        if order[index][1] < far - 1:
+            at_spots(ends, lambda spot: deep_chain(spot, index))
 
     for index in range(pieces):
-        partial(0, index)
-        core_copy(0, index).start()
+        if order[index] == (1, 0) or (far == 1 and index == 1):
+            @pl.when(section == 0)
+            def values_last():
+                to_values(unit_rows_at(units - 1))
+
+        for turn in range(2):
+            partial(turn, index)
+            core_copy(turn, index).start()
         if index > 0:
-            send_side(index - 1)
-    for index in range(pieces):
-        partial(1, index)
-        core_copy(1, index).start()
-        if index == 0:
-            send_side(pieces - 1)
-
-    def up_copy(matrix, block):
-        return pltpu.make_async_remote_copy(
-            src_ref=own_s.at[order.index((matrix, rank_of(block)))],
-            dst_ref=low_in.at[matrix, block],
-            send_sem=low_send.at[matrix, block],
-            recv_sem=low_recv.at[matrix, block],
-            device_id={"dp": (me + 4) % group},
-            device_id_type=MESH,
-        )
-
-    def down_copy(matrix, block):
-        return pltpu.make_async_remote_copy(
-            src_ref=own_s.at[order.index((matrix, rank_of(block)))],
-            dst_ref=high_in.at[matrix, block],
-            send_sem=high_send.at[matrix, block],
-            recv_sem=high_recv.at[matrix, block],
-            device_id={"dp": (me + group - 4) % group},
-            device_id_type=MESH,
-        )
-
-    spot_now = [0]
-
-    def rank_of(block):
-        return ranks[spot_now[0]].index(block)
-
-    def chain(spot, indices):
-        spot_now[0] = spot
-        for index in indices:
-            matrix, rank = order[index]
-            block = ranks[spot][rank]
-            core_copy(1, index).wait_recv()
-            side_copy(index).wait_recv()
-            terms = []
-            if block >= spot and spot > 0:
-                up_copy(matrix, block).wait_recv()
-                terms.append(low_in)
-            if block <= spot and spot < far - 1:
-                down_copy(matrix, block).wait_recv()
-                terms.append(high_in)
-
-            def add(part):
-                mine = own_s[index, part].astype(jnp.float32)
-                mine = mine + core_in[1, index, part].astype(jnp.float32)
-                mine = mine + side_in[index, part].astype(jnp.float32)
-                for term in terms:
-                    mine = mine + term[matrix, block, part].astype(jnp.float32)
-                if block == spot:
-                    (proj_out, value_out)[matrix][part] = mine
-                else:
-                    own_s[index, part] = mine.astype(jnp.bfloat16)
-
-            over_block(add)
-            if block > spot:
-                up_copy(matrix, block).start()
-            elif block < spot:
-                down_copy(matrix, block).start()
+            early(index - 1)
+    early(pieces - 1)
+
+    def pass_deep(spot):
+        for index in range(pieces):
+            if order[index][1] < far - 1:
+                deep_chain(spot, index)
+
+    def own_deep(spot):
+        for index in range(pieces):
+            if order[index][1] == far - 1:
+                deep_chain(spot, index)
+
+    at_spots([spot for spot in range(far) if spot not in ends], pass_deep)
 
     def finish(spot):
         spot_now[0] = spot
@@ -691,18 +782,23 @@
             for block in range(far):
                 if block > spot:
                     up_copy(matrix, block).wait_send()
+                    deep_up(matrix, block).wait_send()
                 elif block < spot:
                     down_copy(matrix, block).wait_send()
+                    deep_down(matrix, block).wait_send()
 
     def stage(indices):
-        for spot in range(far):
-            @pl.when(place == spot)
-            def run(spot=spot):
-                chain(spot, indices)
+        def body(spot):
+            for index in indices:
+                chain(spot, index)
+
+        at_spots(range(far), body)
 
     ahead = min(units, pieces - 1)
     for index in range(ahead):
         stage([index])
+        if index == min(OWN_DEEP, ahead - 1):
+            at_spots(range(far), own_deep)
 
         @pl.when(section == 0)
         def tables(index=index):
@@ -734,6 +830,13 @@
     for step in range(1, group):
         table_copy(step).wait_recv()
         sums = sums + tables_in[step - 1]
+    for matrix in range(2):
+        cross_copy(matrix).wait_recv()
+
+        def add_cross(part):
+            outs[matrix][part, deep_lanes] += cross_in[matrix, part].astype(jnp.float32)
+
+        over_block(add_cross)
     for index in range(3):
         table_out[index] = sums[index:index + 1, :lanes]
 
@@ -744,13 +847,17 @@
     for index in range(pieces):
         core_copy(0, index).wait_send()
         core_copy(1, index).wait_send()
-        side_copy(index).wait_send()
+    for matrix in range(2):
+        cross_copy(matrix).wait_send()
     for step in range(1, group):
         table_copy(step).wait_send()
-    for spot in range(far):
-        @pl.when(place == spot)
-        def drain(spot=spot):
-            finish(spot)
+    at_spots(range(far), finish)
+
+
+def place_kernel(value_ref, proj_ref, table_ref, value_out, proj_out, table_out):
+    value_out[...] = value_ref[...]
+    proj_out[...] = proj_ref[...]
+    table_out[...] = table_ref[...]
 
 
 def per_device(
@@ -761,7 +868,7 @@
     group = lax.axis_size("dp")
     per_sample = rows * group // guide_bin.shape[1]
     if (lax.axis_size("section") != 2 or group % 4 or per_sample % rows or rows % 128
-            or width != depth or width % (group * 16)):
+            or width != depth or width % (group * 16) or width < 768):
         return per_device_scan(
             inputs, out_grad, guide_bin, time_step, guide_table, section_table,
             value_weight, proj_weight,
@@ -772,19 +879,22 @@
     hops = count // piece
     block = (width // group, width)
     pieces = 2 * far
+    deep = (block[0], width // 6 // 128 * 128)
+    near = (block[0], width - deep[1])
     lanes = width // group
     vmem = pl.BlockSpec(memory_space=pltpu.VMEM)
     smem = pl.BlockSpec(memory_space=pltpu.SMEM)
     hbm = pl.BlockSpec(memory_space=pl.ANY)
     dma = pltpu.SemaphoreType.DMA
     half = jnp.bfloat16
-    value_sum, proj_sum, table_sum = pl.pallas_call(
+    shapes = (
+        jax.ShapeDtypeStruct(block, jnp.float32),
+        jax.ShapeDtypeStruct(block, jnp.float32),
+        jax.ShapeDtypeStruct((3, 1, lanes), jnp.float32),
+    )
+    sums = pl.pallas_call(
         functools.partial(step_kernel, far),
-        out_shape=(
-            jax.ShapeDtypeStruct(block, jnp.float32),
-            jax.ShapeDtypeStruct(block, jnp.float32),
-            jax.ShapeDtypeStruct((3, 1, lanes), jnp.float32),
-        ),
+        out_shape=shapes,
         in_specs=[smem, smem, vmem, vmem, hbm, hbm, hbm, hbm],
         out_specs=(vmem,) * 3,
         scratch_shapes=[
@@ -803,16 +913,22 @@
             pltpu.VMEM((3, 8, width), jnp.float32),
             pltpu.VMEM((2, pieces) + block, half),
             pltpu.VMEM((2, pieces) + block, half),
-            pltpu.VMEM((pieces,) + block, half),
-            pltpu.VMEM((pieces,) + block, half),
-            pltpu.VMEM((pieces,) + block, half),
-            pltpu.VMEM((2, far) + block, half),
-            pltpu.VMEM((2, far) + block, half),
+            pltpu.VMEM((2, pieces) + block, half),
+            pltpu.VMEM((pieces,) + near, half),
+            pltpu.VMEM((pieces,) + near, half),
+            pltpu.VMEM((2, far) + near, half),
+            pltpu.VMEM((2, far) + near, half),
+            pltpu.VMEM((pieces, 2) + deep, half),
+            pltpu.VMEM((2, far, 2) + deep, half),
+            pltpu.VMEM((2, far, 2) + deep, half),
+            pltpu.VMEM((2,) + deep, half),
+            pltpu.VMEM((2,) + deep, half),
             pltpu.VMEM((group, 8, 128), jnp.float32),
             pltpu.VMEM((group - 1, 8, 128), jnp.float32),
             dma((2 + units,)), dma((hops,)), dma((hops,)), dma((2, pieces)), dma((2, pieces)),
             dma((pieces,)), dma((pieces,)), dma((2, far)), dma((2, far)), dma((2, far)),
-            dma((2, far)), dma((group - 1,)), dma((group - 1,)),
+            dma((2, far)), dma((2, far)), dma((2, far)), dma((2, far)), dma((2, far)),
+            dma((2,)), dma((2,)), dma((group - 1,)), dma((group - 1,)),
         ],
         compiler_params=pltpu.CompilerParams(
             collective_id=0, has_side_effects=True, vmem_limit_bytes=62 * 1024 * 1024
@@ -822,6 +938,9 @@
         section_table.transpose(1, 0, 2), inputs, out_grad,
         value_weight, proj_weight,
     )
+    value_sum, proj_sum, table_sum = pl.pallas_call(
+        place_kernel, out_shape=shapes, in_specs=[vmem] * 3, out_specs=(vmem,) * 3
+    )(*sums)
     return (value_sum[None], proj_sum[None], table_sum.transpose(1, 0, 2))
 
 

time: 115 us -> 109 us (0.948)
  local copies, waits for them, and re-layouts: 5.05 us -> 0 us
    unnamed x3 -> x0, local copies, waits for them, and re-layouts: 5.05 us -> none
    pallas_call x1 -> x2, Pallas kernels: 109 us -> 108 us  [the longest x1 106 us: per_device(): pl.pallas_call(functools.partial(step_kernel, far), out_shape=shapes, in_...]
where the time goes in v3:
time: 109 us
  Pallas kernels  108 us (99%)
    pallas_call x1, Pallas kernels, per_device(): pl.pallas_call(functools.partial(step_kernel, far), out_shape=shapes, in_...  106 us
    pallas_call x1, Pallas kernels, per_device(): pl.pallas_call(place_kernel, out_shape=shapes, in_specs=[vmem] * 3, out_s...  2.29 us

profile of v3, /device:TPU:0, one launch (start us, length us, event | category | flops | bytes accessed | tf_op | source)
XLA Modules:
  0.0 108.8 jit_solution(10052610340559933345)
XLA Ops:
  0.6 105.8 %shard_map.103 = (f32[96,1536]{1,0:T(8,128)}, f32[96,1536]{1,0:T(8,128)}, f32[3,1,96]{2,1,0:T(1,128)}) custom-call(s32[4]{0:T(128)} %bitcast.7, s32[4]{0:T(128)} %bitcast.8, bf16[32,4608]{1,0:T(8,128)(2,1)} %guide_ref.1, f32[3,1,1536]{2,1,0:T(1,128)} %bitcast.6, bf16[4,128,1536]{2,1,0:T(8,128)(2,1)} %x_hbm.1, bf16[4,128,1536]{2,1,0:T(8,128)(2,1)} %up_hbm.1, ...), custom_call_target="tpu_custom_call" | custom-call | tf_op jit(solution)/shard_map/pallas_call | solution.py:895
  106.5 2.3 %shard_map.104 = (f32[96,1536]{1,0:T(8,128)}, f32[96,1536]{1,0:T(8,128)}, f32[3,1,96]{2,1,0:T(1,128)}) custom-call(f32[96,1536]{1,0:T(8,128)} %get-tuple-element.9.value_ref, f32[96,1536]{1,0:T(8,128)} %get-tuple-element.10.proj_ref, f32[3,1,96]{2,1,0:T(1,128)} %get-tuple-element.11.table_ref), custom_call_target="tpu_custom_call" | custom-call | tf_op jit(solution)/shard_map/pallas_call | solution.py:941

commit v4 on v3

--- a/solution.py
+++ b/solution.py
@@ -15,6 +15,7 @@
 UNROLL = 2
 TILE = 1536
 OWN_DEEP = 2
+TABLES_AHEAD = 1
 
 
 def shifted(value, axis, steps):
@@ -240,12 +241,12 @@
 MESH = pl.DeviceIdType.MESH
 
 
-def step_kernel(far, bin_ref, time_ref, guide_ref, section_ref, x_hbm, up_hbm, wv_hbm, wp_hbm,
-                value_out, proj_out, table_out,
+def step_kernel(far, bin_ref, time_ref, guide_hbm, section_ref, x_hbm, up_hbm, wv_hbm, wp_hbm,
+                value_out, proj_out, table_out, guide_ref,
                 local_s, wv_s, wp_s, rows_s, arrive_s, send_s, mod_s, val_s, left_s, right_s,
-                wide_s, part_s, tab_s, core_out, core_in, kept_s, side_out, side_in, low_in, high_in,
+                wide_s, part_s, tab_s, made_s, core_in, side_out, side_in, low_in, high_in,
                 deep_s, deep_low, deep_high, cross_out, cross_in,
-                tables_s, tables_in, load_sem, hop_send, hop_recv, core_send, core_recv,
+                tables_s, tables_in, small_sem, load_sem, hop_send, hop_recv, core_send, core_recv,
                 side_send, side_recv, low_send, low_recv, high_send, high_recv,
                 down_send, down_recv, rise_send, rise_recv, cross_send, cross_recv,
                 table_send, table_recv):
@@ -260,14 +261,8 @@
     me = lax.axis_index("dp")
     core, side, place = me % 2, (me // 2) % 2, me // 4
 
-    barrier = pltpu.get_barrier_semaphore()
-    pl.semaphore_signal(
-        barrier, inc=1, device_id={"section": 1 - section}, device_id_type=MESH
-    )
-    for step in range(1, group):
-        pl.semaphore_signal(
-            barrier, inc=1, device_id={"dp": (me + step) % group}, device_id_type=MESH
-        )
+    load_guide = pltpu.make_async_copy(guide_hbm, guide_ref, small_sem.at[0])
+    load_guide.start()
 
     def load_rows(source, unit):
         part = pl.ds(unit * unit_rows, unit_rows)
@@ -292,6 +287,16 @@
         for unit in range(1, units):
             load_rows(up_hbm, unit).start()
 
+    barrier = pltpu.get_barrier_semaphore()
+    pl.semaphore_signal(
+        barrier, inc=1, device_id={"section": 1 - section}, device_id_type=MESH
+    )
+    for step in range(1, group):
+        pl.semaphore_signal(
+            barrier, inc=1, device_id={"dp": (me + step) % group}, device_id_type=MESH
+        )
+
+    load_guide.wait()
     total = guide_ref.shape[1]
     half = total // 2
     samples = bin_ref.shape[0] // units
@@ -447,14 +452,16 @@
         load_value.wait()
         size = math.gcd(unit_rows, FORWARD_ROWS)
 
-        @pl.loop(0, count // size)
-        def out(index):
-            forward(index, size)
+        @pl.loop(0, units)
+        def out(unit):
+            @pl.loop(0, unit_rows // size)
+            def some(at):
+                forward(unit * (unit_rows // size) + at, size)
+
+            turn_left(unit)
 
         @pl.loop(0, units)
         def back(unit):
-            turn_left(unit)
-
             @pl.loop(0, per_unit)
             def one(at):
                 receive(unit * per_unit + at)
@@ -462,6 +469,10 @@
             @pl.when(unit < units - 1)
             def values_now():
                 to_values(unit_rows_at(unit))
+
+            @pl.when(unit < min(TABLES_AHEAD, units - 1))
+            def tables_now():
+                table_rows(unit)
 
     def grads_ahead(unit):
         def body(part, unused):
@@ -542,20 +553,17 @@
                 @pl.when((at == 2 % per_unit) & (unit >= 1))
                 def job_values():
                     values_behind(unit - 1)
-
-                @pl.when((at == 3 % per_unit) & (unit >= 1))
+                    turn_left(unit - 1)
+
+                @pl.when((at == 3 % per_unit) & (unit >= 1) & (unit < units - 1))
                 def job_gates():
                     gates_behind(unit - 1)
 
         values_behind(units - 1)
-        gates_behind(units - 1)
-
-        @pl.loop(0, units)
-        def turn(unit):
-            turn_left(unit)
+        turn_left(units - 1)
 
     ranks = [sorted(range(far), key=lambda block: -abs(block - spot)) for spot in range(far)]
-    order = [(0, rank) for rank in range(far - 1)] + [(1, rank) for rank in range(far - 1)]
+    order = [(matrix, rank) for rank in range(far - 1) for matrix in range(2)]
     order = order + [(0, far - 1), (1, far - 1)]
     pieces = len(order)
     block_rows = left_s.shape[1] // group
@@ -577,21 +585,12 @@
         product = jnp.dot(
             left_s[matrix, pl.ds(first, 2 * block_rows)], right_s[matrix],
             preferred_element_type=jnp.float32,
-        ).astype(jnp.bfloat16)
-
-        @pl.when(core == 0)
-        def even():
-            kept_s[turn, index] = product[:block_rows]
-            core_out[turn, index] = product[block_rows:]
-
-        @pl.when(core == 1)
-        def odd():
-            kept_s[turn, index] = product[block_rows:]
-            core_out[turn, index] = product[:block_rows]
+        )
+        made_s[turn, index] = product.astype(jnp.bfloat16).reshape(2, block_rows, width)
 
     def core_copy(turn, index):
         return pltpu.make_async_remote_copy(
-            src_ref=core_out.at[turn, index],
+            src_ref=made_s.at[turn, index, 1 - core],
             dst_ref=core_in.at[turn, index],
             send_sem=core_send.at[turn, index],
             recv_sem=core_recv.at[turn, index],
@@ -658,7 +657,7 @@
     outs = (proj_out, value_out)
 
     def core_sum(turn, index, part, lanes):
-        mine = kept_s[turn, index, part, lanes].astype(jnp.float32)
+        mine = made_s[turn, index, core, part, lanes].astype(jnp.float32)
         return mine + core_in[turn, index, part, lanes].astype(jnp.float32)
 
     def send_side(index):
@@ -752,7 +751,7 @@
             at_spots(ends, lambda spot: deep_chain(spot, index))
 
     for index in range(pieces):
-        if order[index] == (1, 0) or (far == 1 and index == 1):
+        if index == 1:
             @pl.when(section == 0)
             def values_last():
                 to_values(unit_rows_at(units - 1))
@@ -800,10 +799,20 @@
         if index == min(OWN_DEEP, ahead - 1):
             at_spots(range(far), own_deep)
 
+        last = index == ahead - 1
+        behind = (index + TABLES_AHEAD) % units
+        spare = [behind] if ahead == units else range(index, units if last else index + 1)
+
         @pl.when(section == 0)
-        def tables(index=index):
-            for unit in range(index, units if index == ahead - 1 else index + 1):
-                table_rows(unit)
+        def tables(spare=spare):
+            for unit in spare:
+                if unit >= min(TABLES_AHEAD, units - 1):
+                    table_rows(unit)
+
+        @pl.when(section == 1)
+        def gates(index=index):
+            if index < min(2, units):
+                gates_behind(units - 1 - index)
 
     lanes = table_out.shape[2]
     table = jnp.concatenate(
@@ -825,11 +834,14 @@
 
     for step in range(1, group):
         table_copy(step).start()
-    stage(range(ahead, pieces))
+    stage(range(ahead, pieces - 2))
     sums = tables_s[me]
     for step in range(1, group):
         table_copy(step).wait_recv()
         sums = sums + tables_in[step - 1]
+    for row in range(3):
+        table_out[row] = sums[row:row + 1, :lanes]
+    stage(range(max(ahead, pieces - 2), pieces))
     for matrix in range(2):
         cross_copy(matrix).wait_recv()
 
@@ -837,8 +849,6 @@
             outs[matrix][part, deep_lanes] += cross_in[matrix, part].astype(jnp.float32)
 
         over_block(add_cross)
-    for index in range(3):
-        table_out[index] = sums[index:index + 1, :lanes]
 
     @pl.loop(0, hops)
     def sent(index):
@@ -895,9 +905,10 @@
     sums = pl.pallas_call(
         functools.partial(step_kernel, far),
         out_shape=shapes,
-        in_specs=[smem, smem, vmem, vmem, hbm, hbm, hbm, hbm],
+        in_specs=[smem, smem, hbm, vmem, hbm, hbm, hbm, hbm],
         out_specs=(vmem,) * 3,
         scratch_shapes=[
+            pltpu.VMEM(guide_table.shape, guide_table.dtype),
             pltpu.VMEM((count, width), half),
             pltpu.VMEM((width, depth), half),
             pltpu.VMEM((depth, width), half),
@@ -911,8 +922,7 @@
             pltpu.VMEM((count, width), jnp.float32),
             pltpu.VMEM((rows, width), jnp.float32),
             pltpu.VMEM((3, 8, width), jnp.float32),
-            pltpu.VMEM((2, pieces) + block, half),
-            pltpu.VMEM((2, pieces) + block, half),
+            pltpu.VMEM((2, pieces, 2) + block, half),
             pltpu.VMEM((2, pieces) + block, half),
             pltpu.VMEM((pieces,) + near, half),
             pltpu.VMEM((pieces,) + near, half),
@@ -925,7 +935,7 @@
             pltpu.VMEM((2,) + deep, half),
             pltpu.VMEM((group, 8, 128), jnp.float32),
             pltpu.VMEM((group - 1, 8, 128), jnp.float32),
-            dma((2 + units,)), dma((hops,)), dma((hops,)), dma((2, pieces)), dma((2, pieces)),
+            dma((1,)), dma((2 + units,)), dma((hops,)), dma((hops,)), dma((2, pieces)), dma((2, pieces)),
             dma((pieces,)), dma((pieces,)), dma((2, far)), dma((2, far)), dma((2, far)),
             dma((2, far)), dma((2, far)), dma((2, far)), dma((2, far)), dma((2, far)),
             dma((2,)), dma((2,)), dma((group - 1,)), dma((group - 1,)),

time: 109 us -> 107 us (0.982)
  Pallas kernels: 108 us -> 106 us
    pallas_call x1, Pallas kernels: 106 us -> 103 us  [per_device(): pl.pallas_call(functools.partial(step_kernel, far), out_shape=shapes, in_...]
where the time goes in v4:
time: 107 us; the launch traced here: 106 us
  Pallas kernels  106 us (99%)
    pallas_call x1, Pallas kernels, per_device(): pl.pallas_call(functools.partial(step_kernel, far), out_shape=shapes, in_...  103 us
    pallas_call x1, Pallas kernels, per_device(): pl.pallas_call(place_kernel, out_shape=shapes, in_specs=[vmem] * 3, out_s...  2.29 us

profile of v4, /device:TPU:0, one launch (start us, length us, event | category | flops | bytes accessed | tf_op | source)
XLA Modules:
  0.0 106.3 jit_solution(9571163544162371125)
XLA Ops:
  0.6 103.4 %shard_map.103 = (f32[96,1536]{1,0:T(8,128)}, f32[96,1536]{1,0:T(8,128)}, f32[3,1,96]{2,1,0:T(1,128)}) custom-call(s32[4]{0:T(128)} %bitcast.7, s32[4]{0:T(128)} %bitcast.8, bf16[32,4608]{1,0:T(8,128)(2,1)} %guide_hbm.1, f32[3,1,1536]{2,1,0:T(1,128)} %bitcast.6, bf16[4,128,1536]{2,1,0:T(8,128)(2,1)} %x_hbm.1, bf16[4,128,1536]{2,1,0:T(8,128)(2,1)} %up_hbm.1, ...), custom_call_target="tpu_custom_call" | custom-call | tf_op jit(solution)/shard_map/pallas_call | solution.py:905
  104.0 2.3 %shard_map.104 = (f32[96,1536]{1,0:T(8,128)}, f32[96,1536]{1,0:T(8,128)}, f32[3,1,96]{2,1,0:T(1,128)}) custom-call(f32[96,1536]{1,0:T(8,128)} %get-tuple-element.9.value_ref, f32[96,1536]{1,0:T(8,128)} %get-tuple-element.10.proj_ref, f32[3,1,96]{2,1,0:T(1,128)} %get-tuple-element.11.table_ref), custom_call_target="tpu_custom_call" | custom-call | tf_op jit(solution)/shard_map/pallas_call | solution.py:951

commit v5 on v4

--- a/solution.py
+++ b/solution.py
@@ -553,14 +553,12 @@
                 @pl.when((at == 2 % per_unit) & (unit >= 1))
                 def job_values():
                     values_behind(unit - 1)
-                    turn_left(unit - 1)
-
-                @pl.when((at == 3 % per_unit) & (unit >= 1) & (unit < units - 1))
-                def job_gates():
-                    gates_behind(unit - 1)
 
         values_behind(units - 1)
-        turn_left(units - 1)
+
+        @pl.loop(0, units)
+        def turn(unit):
+            turn_left(unit)
 
     ranks = [sorted(range(far), key=lambda block: -abs(block - spot)) for spot in range(far)]
     order = [(matrix, rank) for rank in range(far - 1) for matrix in range(2)]
@@ -811,8 +809,8 @@
 
         @pl.when(section == 1)
         def gates(index=index):
-            if index < min(2, units):
-                gates_behind(units - 1 - index)
+            for unit in range(index, units if last else index + 1):
+                gates_behind(unit)
 
     lanes = table_out.shape[2]
     table = jnp.concatenate(

time: 107 us -> 107 us (level)
  no operation moved by 1% of the time
where the time goes in v5:
time: 107 us; the launch traced here: 106 us
  Pallas kernels  106 us (99%)
    pallas_call x1, Pallas kernels, per_device(): pl.pallas_call(functools.partial(step_kernel, far), out_shape=shapes, in_...  103 us
    pallas_call x1, Pallas kernels, per_device(): pl.pallas_call(place_kernel, out_shape=shapes, in_specs=[vmem] * 3, out_s...  2.29 us

profile of v5, /device:TPU:0, one launch (start us, length us, event | category | flops | bytes accessed | tf_op | source)
XLA Modules:
  0.0 106.3 jit_solution(10126691718622554500)
XLA Ops:
  0.6 103.4 %shard_map.103 = (f32[96,1536]{1,0:T(8,128)}, f32[96,1536]{1,0:T(8,128)}, f32[3,1,96]{2,1,0:T(1,128)}) custom-call(s32[4]{0:T(128)} %bitcast.7, s32[4]{0:T(128)} %bitcast.8, bf16[32,4608]{1,0:T(8,128)(2,1)} %guide_hbm.1, f32[3,1,1536]{2,1,0:T(1,128)} %bitcast.6, bf16[4,128,1536]{2,1,0:T(8,128)(2,1)} %x_hbm.1, bf16[4,128,1536]{2,1,0:T(8,128)(2,1)} %up_hbm.1, ...), custom_call_target="tpu_custom_call" | custom-call | tf_op jit(solution)/shard_map/pallas_call | solution.py:903
  104.0 2.3 %shard_map.104 = (f32[96,1536]{1,0:T(8,128)}, f32[96,1536]{1,0:T(8,128)}, f32[3,1,96]{2,1,0:T(1,128)}) custom-call(f32[96,1536]{1,0:T(8,128)} %get-tuple-element.9.value_ref, f32[96,1536]{1,0:T(8,128)} %get-tuple-element.10.proj_ref, f32[3,1,96]{2,1,0:T(1,128)} %get-tuple-element.11.table_ref), custom_call_target="tpu_custom_call" | custom-call | tf_op jit(solution)/shard_map/pallas_call | solution.py:949
